TPU v7x, 32 devices: a 4x4x1 block of a 4x4x8 slice. The times are simulated.
32 devices in a mesh: pod: 1 (over z), dp: 4 (over y), sp: 8 (over x, core).
Axes of the slice: x: 4, y: 4, z: 1, core: 2. Of those that a mesh axis runs over, the one named last changes fastest.
The devices are a block of a 4x4x8 slice.
Arguments:
- images: bfloat16 [48, 256, 56, 64], P(('pod', 'dp'), 'sp')
- w_a: bfloat16 [2, 3, 3, 64, 64], replicated
- norm_a: float32 [2, 2, 64], replicated
- w_down: bfloat16 [3, 3, 64, 128], replicated
- norm_down: float32 [2, 128], replicated
- w_b: bfloat16 [2, 3, 3, 128, 128], replicated
- norm_b: float32 [2, 2, 128], replicated
Outputs:
- output: bfloat16 [48, 128, 28, 128], P(('pod', 'dp'), 'sp')
All inputs are finite; a program needn't handle non-finite values.
Results may differ from a plain program's by a relative error of at most 0.0039231.
Values are sent between devices in bfloat16 or wider.
A program may use at most 768 MiB of HBM per device.

v0:
```python
import jax
import jax.numpy as jnp
from jax import lax
from jax.sharding import PartitionSpec as P

EPS_VALUE = 1e-5
CONV_DIMS = ('NHWC', 'HWIO', 'NHWC')


def solution(mesh):
    group_size = mesh.shape['sp']
    data_size = mesh.shape['dp']
    to_lower = [(dev_idx, dev_idx + 1) for dev_idx in range(group_size - 1)]
    to_upper = [(dev_idx + 1, dev_idx) for dev_idx in range(group_size - 1)]

    def batch_norm(z_val, norm_pair):
        local_sums = jnp.stack([jnp.sum(z_val, axis=(0, 1, 2)), jnp.sum(z_val * z_val, axis=(0, 1, 2))])
        group_sums = lax.psum(local_sums, ('dp', 'sp'))
        elem_count = z_val.shape[0] * z_val.shape[1] * z_val.shape[2] * data_size * group_size
        mean_val = group_sums[0] / elem_count
        var_val = group_sums[1] / elem_count - mean_val * mean_val
        scaled = norm_pair[0] * (z_val - mean_val) * lax.rsqrt(var_val + EPS_VALUE) + norm_pair[1]
        return jnp.maximum(scaled, 0.0).astype(jnp.bfloat16)

    def same_layer(hidden, weight, norm_pair):
        top_rows = lax.ppermute(hidden[:, -1:], 'sp', to_lower)
        bottom_rows = lax.ppermute(hidden[:, :1], 'sp', to_upper)
        padded = jnp.concatenate([top_rows, hidden, bottom_rows], axis=1)
        z_val = lax.conv_general_dilated(padded, weight, (1, 1), ((0, 0), (1, 1)), dimension_numbers=CONV_DIMS, preferred_element_type=jnp.float32)
        return batch_norm(z_val, norm_pair)

    def down_layer(hidden, weight, norm_pair):
        bottom_rows = lax.ppermute(hidden[:, :1], 'sp', to_upper)
        padded = jnp.concatenate([hidden, bottom_rows], axis=1)
        z_val = lax.conv_general_dilated(padded, weight, (2, 2), ((0, 0), (0, 1)), dimension_numbers=CONV_DIMS, preferred_element_type=jnp.float32)
        return batch_norm(z_val, norm_pair)

    def local_stack(row_tile, w_a, norm_a, w_down, norm_down, w_b, norm_b):
        hidden = row_tile
        for layer_idx in range(w_a.shape[0]):
            hidden = same_layer(hidden, w_a[layer_idx], norm_a[layer_idx])
        hidden = down_layer(hidden, w_down, norm_down)
        for layer_idx in range(w_b.shape[0]):
            hidden = same_layer(hidden, w_b[layer_idx], norm_b[layer_idx])
        return hidden

    act_spec = P(('pod', 'dp'), 'sp', None, None)
    return jax.shard_map(local_stack, mesh=mesh, in_specs=(act_spec, P(), P(), P(), P(), P(), P()), out_specs=act_spec, check_vma=False)
```

profile of v0, /device:TPU:97, one launch (start us, length us, event | category | flops | bytes accessed | tf_op | source)
XLA Modules:
  0.0 364.3 jit_solution(2698824143278537531)
XLA Ops:
  0.0 0.0 copy-start
  0.0 0.0 copy-start.1
  0.0 0.0 copy-start.5
  0.0 8.3 %copy.8 = bf16[12,32,56,64]{3,0,2,1:T(8,128)(2,1)S(1)} copy(bf16[12,32,56,64]{3,2,1,0:T(8,128)(2,1)} %param.7) | data formatting | bytes 5505024 | tf_op args[0]
  8.3 4.6 %collective-permute-start = (bf16[12,1,56,64]{3,0,2,1:T(8,128)(2,1)S(1)}, bf16[12,1,56,64]{3,0,2,1:T(8,128)(2,1)S(1)}, u32[]{:S(2)}, u32[]{:S(2)}) collective-permute-start(bf16[12,1,56,64]{3,0,2,1:T(8,128)(2,1)S(1)} %get-tuple-element.17), channel_id=1, source_target_pairs={{0,1},{1,2},{2,3},{3,4},{4,5},{5,6},{6,7},{8,9},{9,10},{10,11},{11... | collective-permute-start | bytes 258056 | tf_op jit(solution)/shard_map/ppermute | solution.py:26
  12.9 2.1 collective-permute-start.1
  15.1 0.0 copy-done.1
  15.1 0.8 collective-permute-done
  15.9 4.4 %collective-permute-done.1 = bf16[12,1,56,64]{3,0,2,1:T(8,128)(2,1)S(1)} collective-permute-done((bf16[12,1,56,64]{3,0,2,1:T(8,128)(2,1)S(1)}, bf16[12,1,56,64]{3,0,2,1:T(8,128)(2,1)S(1)}, u32[]{:S(2)}, u32[]{:S(2)}) %collective-permute-start.1) | collective-permute-done | bytes 86048 | tf_op jit(solution)/shard_map/ppermute | solution.py:27
  20.3 0.0 copy-done.5
  20.3 13.2 %fusion.52 = (f32[64]{0:T(128)S(1)}, f32[64]{0:T(128)S(1)}, f32[12,32,56,64]{3,0,2,1:T(8,128)}) fusion(bf16[2,3,3,64,64]{4,3,2,1,0:T(8,128)(2,1)S(1)} %copy-done.5, bf16[12,1,56,64]{3,0,2,1:T(8,128)(2,1)S(1)} %collective-permute-done.1, bf16[12,32,56,64]{3,0,2,1:T(8,128)(2,1)S(1)} %copy.8, bf16[12,1,56,64]{3,0,2,1:T(8,128)(2,1)S(1)} %collective-permute-done), kind=kOutput, calls=%fused_computation.87 | convolution fusion | flops 1579474944 | bytes 13451776 | tf_op jit(solution)/shard_map/conv_general_dilated | solution.py:29
  33.5 47.4 %psum.35 = f32[2,64]{1,0:T(2,128)S(1)} all-reduce(f32[2,64]{1,0:T(2,128)S(1)} %pad_maximum_fusion), channel_id=1, replica_groups=mesh['pod'=1,'dp'=4,'sp'=8] {'dp','sp'}, use_global_device_ids=true, to_apply=%region_2.0 | all-reduce | flops 128 | bytes 1024 | tf_op jit(solution)/shard_map/psum | solution.py:18
  81.0 11.2 %maximum_convert_fusion.1 = bf16[12,32,56,64]{3,0,2,1:T(8,128)(2,1)} fusion(f32[12,32,56,64]{3,0,2,1:T(8,128)} %get-tuple-element.33, f32[64]{0:T(128)S(1)} %get-tuple-element.30, f32[64]{0:T(128)S(1)} %fusion.45, f32[64]{0:T(128)S(1)} %multiply_bitcast_fusion.4, f32[64]{0:T(128)S(1)} %get-tuple-element.28), kind=kLoop, calls=%fused_computation.2 | loop fusion | flops 8257536 | bytes 8258560 | tf_op jit(solution)/shard_map/convert_element_type | solution.py:23
  92.2 1.1 fusion.56
  93.3 3.0 collective-permute-start.2
  96.3 2.2 collective-permute-start.3
  98.5 0.8 collective-permute-done.2
  99.2 4.4 %collective-permute-done.3 = bf16[12,1,56,64]{3,0,2,1:T(8,128)(2,1)S(1)} collective-permute-done((bf16[12,1,56,64]{3,0,2,1:T(8,128)(2,1)S(1)}, bf16[12,1,56,64]{3,0,2,1:T(8,128)(2,1)S(1)}, u32[]{:S(2)}, u32[]{:S(2)}) %collective-permute-start.3) | collective-permute-done | bytes 86048 | tf_op jit(solution)/shard_map/ppermute | solution.py:27
  103.7 15.3 %fusion.51 = (f32[64]{0:T(128)S(1)}, f32[64]{0:T(128)S(1)}, f32[12,32,56,64]{3,0,2,1:T(8,128)}) fusion(bf16[2,3,3,64,64]{4,3,2,1,0:T(8,128)(2,1)S(1)} %copy-done.5, bf16[12,1,56,64]{3,0,2,1:T(8,128)(2,1)S(1)} %collective-permute-done.3, bf16[12,32,56,64]{3,0,2,1:T(8,128)(2,1)} %maximum_convert_fusion.1, bf16[12,1,56,64]{3,0,2,1:T(8,128)(2,1)S(1)} %collective-permute-done.2), kind=kOutput, calls=%fused_computation.86 | convolution fusion | flops 1579474944 | bytes 8864256 | tf_op jit(solution)/shard_map/conv_general_dilated | solution.py:29
  119.0 44.4 %psum.36 = f32[2,64]{1,0:T(2,128)S(1)} all-reduce(f32[2,64]{1,0:T(2,128)S(1)} %pad_maximum_fusion.1), channel_id=1, replica_groups=mesh['pod'=1,'dp'=4,'sp'=8] {'dp','sp'}, use_global_device_ids=true, to_apply=%region_5.0 | all-reduce | flops 128 | bytes 1024 | tf_op jit(solution)/shard_map/psum | solution.py:18
  163.4 0.0 copy-start.3
  163.5 11.3 %maximum_convert_fusion = bf16[12,32,56,64]{3,0,2,1:T(8,128)(2,1)} fusion(f32[12,32,56,64]{3,0,2,1:T(8,128)} %get-tuple-element.34, f32[64]{0:T(128)S(1)} %get-tuple-element.29, f32[64]{0:T(128)S(1)} %fusion.43, f32[64]{0:T(128)S(1)} %multiply_bitcast_fusion.3, f32[64]{0:T(128)S(1)} %get-tuple-element.27), kind=kLoop, calls=%fused_computation | loop fusion | flops 8257536 | bytes 8258560 | tf_op jit(solution)/shard_map/convert_element_type | solution.py:23
  174.7 1.0 slice.156
  175.7 3.3 collective-permute-start.4
  179.0 0.0 copy-done.3
  179.0 4.0 %collective-permute-done.4 = bf16[12,1,56,64]{3,0,2,1:T(8,128)(2,1)S(1)} collective-permute-done((bf16[12,1,56,64]{3,0,2,1:T(8,128)(2,1)S(1)}, bf16[12,1,56,64]{3,0,2,1:T(8,128)(2,1)S(1)}, u32[]{:S(2)}, u32[]{:S(2)}) %collective-permute-start.4) | collective-permute-done | bytes 86048 | tf_op jit(solution)/shard_map/ppermute | solution.py:33
  183.0 0.0 copy-done
  183.0 8.0 %fusion.55 = (f32[128]{0:T(128)S(1)}, f32[128]{0:T(128)S(1)}, f32[12,16,28,128]{3,0,2,1:T(8,128)}) fusion(bf16[3,3,64,128]{3,2,1,0:T(8,128)(2,1)S(1)} %copy-done, bf16[12,1,56,64]{3,0,2,1:T(8,128)(2,1)S(1)} %collective-permute-done.4, bf16[12,32,56,64]{3,0,2,1:T(8,128)(2,1)} %maximum_convert_fusion), kind=kOutput, calls=%fused_computation.90 | convolution fusion | flops 791027456 | bytes 5739520 | tf_op jit(solution)/shard_map/conv_general_dilated | solution.py:35
  191.0 0.0 copy-start.2
  191.0 0.0 copy-start.4
  191.1 43.2 %psum.37 = f32[2,128]{1,0:T(2,128)S(1)} all-reduce(f32[2,128]{1,0:T(2,128)S(1)} %pad_maximum_fusion.2), channel_id=1, replica_groups=mesh['pod'=1,'dp'=4,'sp'=8] {'dp','sp'}, use_global_device_ids=true, to_apply=%region_8.0 | all-reduce | flops 256 | bytes 2048 | tf_op jit(solution)/shard_map/psum | solution.py:18
  234.3 2.8 maximum_convert_fusion.4
  237.2 3.4 collective-permute-start.5
  240.6 2.0 collective-permute-start.6
  242.5 0.0 copy-done.2
  242.5 0.0 collective-permute-done.5
  242.6 4.1 %collective-permute-done.6 = bf16[12,1,28,128]{3,0,2,1:T(8,128)(2,1)S(1)} collective-permute-done((bf16[12,1,28,128]{3,0,2,1:T(8,128)(2,1)S(1)}, bf16[12,1,28,128]{3,0,2,1:T(8,128)(2,1)S(1)}, u32[]{:S(2)}, u32[]{:S(2)}) %collective-permute-start.6) | collective-permute-done | bytes 86048 | tf_op jit(solution)/shard_map/ppermute | solution.py:27
  246.7 0.0 copy-done.4
  246.7 6.3 %fusion.54 = (f32[128]{0:T(128)S(1)}, f32[128]{0:T(128)S(1)}, f32[12,16,28,128]{3,0,2,1:T(8,128)}) fusion(bf16[2,3,3,128,128]{4,3,2,1,0:T(8,128)(2,1)S(1)} %copy-done.4, bf16[12,1,28,128]{3,0,2,1:T(8,128)(2,1)S(1)} %collective-permute-done.6, bf16[12,16,28,128]{3,0,2,1:T(8,128)(2,1)S(1)} %maximum_convert_fusion.4, ...), kind=kOutput, calls=%fused_computation.89 | convolution fusion | flops 1554407168 | bytes 5112832 | tf_op jit(solution)/shard_map/conv_general_dilated | solution.py:29
  253.0 44.5 %psum.38 = f32[2,128]{1,0:T(2,128)S(1)} all-reduce(f32[2,128]{1,0:T(2,128)S(1)} %pad_maximum_fusion.3), channel_id=1, replica_groups=mesh['pod'=1,'dp'=4,'sp'=8] {'dp','sp'}, use_global_device_ids=true, to_apply=%region_11.0 | all-reduce | flops 256 | bytes 2048 | tf_op jit(solution)/shard_map/psum | solution.py:18
  297.5 2.8 maximum_convert_fusion.3
  300.3 2.1 collective-permute-start.7
  302.5 2.4 collective-permute-start.8
  304.9 0.0 collective-permute-done.7
  304.9 3.7 %collective-permute-done.8 = bf16[12,1,28,128]{3,0,2,1:T(8,128)(2,1)S(1)} collective-permute-done((bf16[12,1,28,128]{3,0,2,1:T(8,128)(2,1)S(1)}, bf16[12,1,28,128]{3,0,2,1:T(8,128)(2,1)S(1)}, u32[]{:S(2)}, u32[]{:S(2)}) %collective-permute-start.8) | collective-permute-done | bytes 86048 | tf_op jit(solution)/shard_map/ppermute | solution.py:27
  308.6 6.3 %fusion.53 = (f32[128]{0:T(128)S(1)}, f32[128]{0:T(128)S(1)}, f32[12,16,28,128]{3,0,2,1:T(8,128)}) fusion(bf16[2,3,3,128,128]{4,3,2,1,0:T(8,128)(2,1)S(1)} %copy-done.4, bf16[12,1,28,128]{3,0,2,1:T(8,128)(2,1)S(1)} %collective-permute-done.8, bf16[12,16,28,128]{3,0,2,1:T(8,128)(2,1)S(1)} %maximum_convert_fusion.3, ...), kind=kOutput, calls=%fused_computation.88 | convolution fusion | flops 1554407168 | bytes 5112832 | tf_op jit(solution)/shard_map/conv_general_dilated | solution.py:29
  314.9 44.4 %psum.39 = f32[2,128]{1,0:T(2,128)S(1)} all-reduce(f32[2,128]{1,0:T(2,128)S(1)} %pad_maximum_fusion.4), channel_id=1, replica_groups=mesh['pod'=1,'dp'=4,'sp'=8] {'dp','sp'}, use_global_device_ids=true, to_apply=%region_14.0 | all-reduce | flops 256 | bytes 2048 | tf_op jit(solution)/shard_map/psum | solution.py:18
  359.3 2.8 maximum_convert_fusion.2
  362.1 2.0 copy.11
  (21 shorter events, 0.2 us)
Async XLA Ops:
  0.0 183.0 %copy-start = (bf16[3,3,64,128]{3,2,1,0:T(8,128)(2,1)S(1)}, bf16[3,3,64,128]{3,2,1,0:T(8,128)(2,1)}, u32[]{:S(2)}) copy-start(bf16[3,3,64,128]{3,2,1,0:T(8,128)(2,1)} %param.10) | copy-start | bytes 442372
  0.0 15.1 %copy-start.1 = (f32[2,2,64]{2,1,0:T(2,128)S(1)}, f32[2,2,64]{2,1,0:T(2,128)}, u32[]{:S(2)}) copy-start(f32[2,2,64]{2,1,0:T(2,128)} %param.9) | copy-start | bytes 3076
  0.0 20.3 %copy-start.5 = (bf16[2,3,3,64,64]{4,3,2,1,0:T(8,128)(2,1)S(1)}, bf16[2,3,3,64,64]{4,3,2,1,0:T(8,128)(2,1)}, u32[]{:S(2)}) copy-start(bf16[2,3,3,64,64]{4,3,2,1,0:T(8,128)(2,1)} %param.8) | copy-start | bytes 442372
  8.3 7.5 %collective-permute-start = (bf16[12,1,56,64]{3,0,2,1:T(8,128)(2,1)S(1)}, bf16[12,1,56,64]{3,0,2,1:T(8,128)(2,1)S(1)}, u32[]{:S(2)}, u32[]{:S(2)}) collective-permute-start(bf16[12,1,56,64]{3,0,2,1:T(8,128)(2,1)S(1)} %get-tuple-element.17), channel_id=1, source_target_pairs={{0,1},{1,2},{2,3},{3,4},{4,5},{5,6},{6,7},{8,9},{9,10},{10,11},{11... | collective-permute-start | bytes 258056 | tf_op jit(solution)/shard_map/ppermute | solution.py:26
  12.9 7.4 %collective-permute-start.1 = (bf16[12,1,56,64]{3,0,2,1:T(8,128)(2,1)S(1)}, bf16[12,1,56,64]{3,0,2,1:T(8,128)(2,1)S(1)}, u32[]{:S(2)}, u32[]{:S(2)}) collective-permute-start(bf16[12,1,56,64]{3,0,2,1:T(8,128)(2,1)S(1)} %get-tuple-element.18), channel_id=1, source_target_pairs={{1,0},{2,1},{3,2},{4,3},{5,4},{6,5},{7,6},{9,8},{10,9},{11,10},{12... | collective-permute-start | bytes 258056 | tf_op jit(solution)/shard_map/ppermute | solution.py:27
  93.3 5.9 %collective-permute-start.2 = (bf16[12,1,56,64]{3,0,2,1:T(8,128)(2,1)S(1)}, bf16[12,1,56,64]{3,0,2,1:T(8,128)(2,1)S(1)}, u32[]{:S(2)}, u32[]{:S(2)}) collective-permute-start(bf16[12,1,56,64]{3,0,2,1:T(8,128)(2,1)S(1)} %get-tuple-element.15), channel_id=1, source_target_pairs={{0,1},{1,2},{2,3},{3,4},{4,5},{5,6},{6,7},{8,9},{9,10},{10,11},{11... | collective-permute-start | bytes 258056 | tf_op jit(solution)/shard_map/ppermute | solution.py:26
  96.3 7.4 %collective-permute-start.3 = (bf16[12,1,56,64]{3,0,2,1:T(8,128)(2,1)S(1)}, bf16[12,1,56,64]{3,0,2,1:T(8,128)(2,1)S(1)}, u32[]{:S(2)}, u32[]{:S(2)}) collective-permute-start(bf16[12,1,56,64]{3,0,2,1:T(8,128)(2,1)S(1)} %get-tuple-element.16), channel_id=1, source_target_pairs={{1,0},{2,1},{3,2},{4,3},{5,4},{6,5},{7,6},{9,8},{10,9},{11,10},{12... | collective-permute-start | bytes 258056 | tf_op jit(solution)/shard_map/ppermute | solution.py:27
  163.4 15.5 %copy-start.3 = (f32[2,128]{1,0:T(2,128)S(1)}, f32[2,128]{1,0:T(2,128)}, u32[]{:S(2)}) copy-start(f32[2,128]{1,0:T(2,128)} %param.11) | copy-start | bytes 3076
  175.7 7.4 %collective-permute-start.4 = (bf16[12,1,56,64]{3,0,2,1:T(8,128)(2,1)S(1)}, bf16[12,1,56,64]{3,0,2,1:T(8,128)(2,1)S(1)}, u32[]{:S(2)}, u32[]{:S(2)}) collective-permute-start(bf16[12,1,56,64]{3,0,2,1:T(8,128)(2,1)S(1)} %slice.156), channel_id=1, source_target_pairs={{1,0},{2,1},{3,2},{4,3},{5,4},{6,5},{7,6},{9,8},{10,9},{11,10},{12... | collective-permute-start | bytes 258056 | tf_op jit(solution)/shard_map/ppermute | solution.py:33
  191.0 51.5 %copy-start.2 = (f32[2,2,128]{2,1,0:T(2,128)S(1)}, f32[2,2,128]{2,1,0:T(2,128)}, u32[]{:S(2)}) copy-start(f32[2,2,128]{2,1,0:T(2,128)} %param.13) | copy-start | bytes 6148
  191.0 55.7 %copy-start.4 = (bf16[2,3,3,128,128]{4,3,2,1,0:T(8,128)(2,1)S(1)}, bf16[2,3,3,128,128]{4,3,2,1,0:T(8,128)(2,1)}, u32[]{:S(2)}) copy-start(bf16[2,3,3,128,128]{4,3,2,1,0:T(8,128)(2,1)} %param.12) | copy-start | bytes 1769476
  237.2 5.4 %collective-permute-start.5 = (bf16[12,1,28,128]{3,0,2,1:T(8,128)(2,1)S(1)}, bf16[12,1,28,128]{3,0,2,1:T(8,128)(2,1)S(1)}, u32[]{:S(2)}, u32[]{:S(2)}) collective-permute-start(bf16[12,1,28,128]{3,0,2,1:T(8,128)(2,1)S(1)} %get-tuple-element.21), channel_id=1, source_target_pairs={{0,1},{1,2},{2,3},{3,4},{4,5},{5,6},{6,7},{8,9},{9,10},{10,11},{11... | collective-permute-start | bytes 258056 | tf_op jit(solution)/shard_map/ppermute | solution.py:26
  240.6 6.1 %collective-permute-start.6 = (bf16[12,1,28,128]{3,0,2,1:T(8,128)(2,1)S(1)}, bf16[12,1,28,128]{3,0,2,1:T(8,128)(2,1)S(1)}, u32[]{:S(2)}, u32[]{:S(2)}) collective-permute-start(bf16[12,1,28,128]{3,0,2,1:T(8,128)(2,1)S(1)} %get-tuple-element.22), channel_id=1, source_target_pairs={{1,0},{2,1},{3,2},{4,3},{5,4},{6,5},{7,6},{9,8},{10,9},{11,10},{12... | collective-permute-start | bytes 258056 | tf_op jit(solution)/shard_map/ppermute | solution.py:27
  300.3 4.6 %collective-permute-start.7 = (bf16[12,1,28,128]{3,0,2,1:T(8,128)(2,1)S(1)}, bf16[12,1,28,128]{3,0,2,1:T(8,128)(2,1)S(1)}, u32[]{:S(2)}, u32[]{:S(2)}) collective-permute-start(bf16[12,1,28,128]{3,0,2,1:T(8,128)(2,1)S(1)} %get-tuple-element.19), channel_id=1, source_target_pairs={{0,1},{1,2},{2,3},{3,4},{4,5},{5,6},{6,7},{8,9},{9,10},{10,11},{11... | collective-permute-start | bytes 258056 | tf_op jit(solution)/shard_map/ppermute | solution.py:26
  302.5 6.1 %collective-permute-start.8 = (bf16[12,1,28,128]{3,0,2,1:T(8,128)(2,1)S(1)}, bf16[12,1,28,128]{3,0,2,1:T(8,128)(2,1)S(1)}, u32[]{:S(2)}, u32[]{:S(2)}) collective-permute-start(bf16[12,1,28,128]{3,0,2,1:T(8,128)(2,1)S(1)} %get-tuple-element.20), channel_id=1, source_target_pairs={{1,0},{2,1},{3,2},{4,3},{5,4},{6,5},{7,6},{9,8},{10,9},{11,10},{12... | collective-permute-start | bytes 258056 | tf_op jit(solution)/shard_map/ppermute | solution.py:27
where the time goes:
time: 370 us; the launch traced here: 364 us
  blocking collectives  224 us (61%)
  matrix products  49 us (13%)
  other arithmetic  31.1 us (8%)
  starting transfers between devices  25.1 us (7%)
  waiting for transfers between devices  22.3 us (6%)
  local copies, waits for them, and re-layouts  12.4 us (3%)
    psum x5, blocking collectives, batch_norm(): group_sums = lax.psum(local_sums, ('dp', 'sp'))  224 us
    conv_general_dilated x4, matrix products, same_layer(): lax.conv_general_dilated(padded, weight, (1, 1), ((0, 0), (1, 1)), dimens...  41 us
    convert_element_type x5, other arithmetic, batch_norm(): return jnp.maximum(scaled, 0.0).astype(jnp.bfloat16)  30.9 us
    ppermute x4, waiting for transfers between devices, same_layer(): bottom_rows = lax.ppermute(hidden[:, :1], 'sp', to_upper)  16.7 us
    ppermute x4, starting transfers between devices, same_layer(): top_rows = lax.ppermute(hidden[:, -1:], 'sp', to_lower)  13.1 us
    ppermute x4, starting transfers between devices, same_layer(): bottom_rows = lax.ppermute(hidden[:, :1], 'sp', to_upper)  8.66 us
    unnamed x13, local copies, waits for them, and re-layouts  8.3 us
    conv_general_dilated x1, matrix products, down_layer(): lax.conv_general_dilated(padded, weight, (2, 2), ((0, 0), (0, 1)), dimens...  8 us
  transfers between devices with their start and end apart: 9, of which 7 were waited for; matrix products, arithmetic and copies ran while one was open for 0% of the time, Pallas kernels for 0%

commit v1 on v0

v1 whole, which is shorter than its diff:
```python
import functools

import jax
import jax.numpy as jnp
from jax import lax
from jax.experimental import pallas as pl
from jax.experimental.pallas import tpu as pltpu
from jax.sharding import PartitionSpec as P

EPS_VALUE = 1e-5
MESH_ID = pl.DeviceIdType.MESH
LANES = 128
HALO = 3
GUARD = 8
F32 = jnp.float32
BF16 = jnp.bfloat16


def stack_kernel(data_size, group_size, images, w_a, norm_a, w_down, norm_down, w_b, norm_b, out,
                 x_in, w_a_in, w_down_in, w_b_in, wide_a, wide_down, wide_b, pixels, masks, taps, z_a, z_down, z_b, z_last,
                 out_rows, parts, slots, in_sems, w_sems, out_sems, image_send, image_recv, z_send, z_recv, sum_send, sum_recv):
    n_img, rows, width, _ = images.shape
    half = width // 2
    block = n_img * half
    pairs = rows // 2
    total = data_size * group_size
    dp_idx = lax.axis_index('dp')
    sp_idx = lax.axis_index('sp')
    me = dp_idx * group_size + sp_idx
    is_top = sp_idx == 0
    is_bottom = sp_idx == group_size - 1

    def peer_of(step):
        other = lax.rem(me + step, total)
        return {'dp': other // group_size, 'sp': lax.rem(other, group_size)}

    barrier = pltpu.get_barrier_semaphore()
    for step in range(1, total):
        pl.semaphore_signal(barrier, inc=1, device_id=peer_of(step), device_id_type=MESH_ID)

    n_chunk = in_sems.shape[0]
    chunk = rows // n_chunk

    def image_copy(idx):
        return pltpu.make_async_copy(images.at[:, pl.ds(idx * chunk, chunk)], x_in.at[:, pl.ds(HALO + idx * chunk, chunk)], in_sems.at[idx])

    for idx in range(n_chunk):
        image_copy(idx).start()
    weight_copies = [pltpu.make_async_copy(w_a, w_a_in, w_sems.at[0]), pltpu.make_async_copy(w_down, w_down_in, w_sems.at[1]),
                     pltpu.make_async_copy(w_b, w_b_in, w_sems.at[2])]
    for copy in weight_copies:
        copy.start()

    pos = lax.rem(lax.broadcasted_iota(jnp.int32, (block, LANES), 0), half)
    masks[0] = (pos != 0).astype(F32)
    masks[1] = (pos != half - 1).astype(F32)
    pixels[0:GUARD] = jnp.zeros((GUARD, LANES), F32)
    pixels[GUARD + n_img * width:] = jnp.zeros((GUARD, LANES), F32)

    def clear_guards(ref, outer):
        def body(idx, carry):
            view = ref.at[idx]
            view[0:GUARD] = jnp.zeros((GUARD, LANES), F32)
            view[GUARD + block:] = jnp.zeros((GUARD, LANES), F32)
            return carry
        lax.fori_loop(0, outer, body, 0)

    clear_guards(z_a, z_a.shape[0])

    def clear_inner(ref):
        def body(idx, carry):
            view = ref.at[idx]
            view[0:GUARD] = jnp.zeros((GUARD, LANES), F32)
            view[GUARD + block:] = jnp.zeros((GUARD, LANES), F32)
            return carry
        lax.fori_loop(1, pairs + 1, body, 0)

    clear_inner(z_down)
    clear_inner(z_b)

    @pl.when(is_top)
    def _():
        x_in[:, 0:HALO] = jnp.zeros((n_img, HALO, width, x_in.shape[3]), BF16)
        z_down[0] = jnp.zeros(z_down.shape[1:], F32)
        z_b[0] = jnp.zeros(z_b.shape[1:], F32)

    @pl.when(is_bottom)
    def _():
        x_in[:, HALO + rows:] = jnp.zeros((n_img, HALO, width, x_in.shape[3]), BF16)
        z_down[pairs + 1] = jnp.zeros(z_down.shape[1:], F32)
        z_b[pairs + 1] = jnp.zeros(z_b.shape[1:], F32)

    pl.semaphore_wait(barrier, total - 1)

    def image_down():
        return pltpu.make_async_remote_copy(src_ref=images.at[:, pl.ds(rows - HALO, HALO)], dst_ref=x_in.at[:, pl.ds(0, HALO)],
                                            send_sem=image_send.at[0], recv_sem=image_recv.at[0],
                                            device_id={'sp': sp_idx + 1}, device_id_type=MESH_ID)

    def image_up():
        return pltpu.make_async_remote_copy(src_ref=images.at[:, pl.ds(0, HALO)], dst_ref=x_in.at[:, pl.ds(HALO + rows, HALO)],
                                            send_sem=image_send.at[1], recv_sem=image_recv.at[1],
                                            device_id={'sp': sp_idx - 1}, device_id_type=MESH_ID)

    @pl.when(jnp.logical_not(is_bottom))
    def _():
        image_down().start()

    @pl.when(jnp.logical_not(is_top))
    def _():
        image_up().start()

    for copy in weight_copies:
        copy.wait()
    ch_a = w_a.shape[3]
    zero_a = jnp.zeros((ch_a, ch_a), BF16)
    zero_b = jnp.zeros((LANES, LANES), BF16)
    zero_d = jnp.zeros((ch_a, LANES), BF16)

    def tap_a(layer, p, q):
        return w_a_in[layer, p, q] if 0 <= p <= 2 and 0 <= q <= 2 else zero_a

    for layer in range(2):
        for q in range(4):
            for t in range(4):
                for dw in range(2):
                    both = jnp.concatenate([tap_a(layer, t, q - dw), tap_a(layer, t - 1, q - dw)], axis=1)
                    wide_a[layer, pl.ds((q * 4 + t) * ch_a, ch_a), pl.ds(dw * LANES, LANES)] = both
    for q in range(3):
        for t in range(6):
            for d in range(2):
                p = t - 1 - 2 * d
                wide_down[pl.ds((q * 6 + t) * ch_a, ch_a), pl.ds(d * LANES, LANES)] = w_down_in[p, q] if 0 <= p <= 2 else zero_d
    for layer in range(2):
        for q in range(3):
            for t in range(4):
                for d in range(2):
                    p = t - d
                    wide_b[layer, pl.ds((q * 4 + t) * LANES, LANES), pl.ds(d * LANES, LANES)] = w_b_in[layer, p, q] if 0 <= p <= 2 else zero_b

    def spread_pair(p, carry):
        upper = x_in[:, 2 * p].astype(F32)
        lower = x_in[:, 2 * p + 1].astype(F32)
        both = jnp.concatenate([upper, lower], axis=2)
        pixels[pl.ds(GUARD, n_img * width)] = both.reshape(n_img * width, LANES)
        taps[0, p] = (pixels[pl.ds(GUARD - 1, block, stride=2)] * masks[0]).astype(BF16)
        taps[1, p] = pixels[pl.ds(GUARD, block, stride=2)].astype(BF16)
        taps[2, p] = pixels[pl.ds(GUARD + 1, block, stride=2)].astype(BF16)
        taps[3, p] = (pixels[pl.ds(GUARD + 2, block, stride=2)] * masks[1]).astype(BF16)
        return carry

    def conv_a(layer, idx):
        left = jnp.concatenate([taps[q, idx + s] for q in range(4) for s in range(2)], axis=1)
        z_val = jnp.dot(left, wide_a[layer], preferred_element_type=F32)
        z_a[idx, pl.ds(GUARD, block)] = z_val[:, :LANES]
        z_a[idx + pairs + 2, pl.ds(GUARD, block)] = z_val[:, LANES:]
        return z_val

    def conv_down(idx):
        left = jnp.concatenate([taps[q, 2 * idx + s] for q in range(1, 4) for s in range(3)], axis=1)
        z_val = jnp.dot(left, wide_down[...], preferred_element_type=F32)
        z_down[2 * idx + 1, pl.ds(GUARD, block)] = z_val[:, :LANES]
        z_down[2 * idx + 2, pl.ds(GUARD, block)] = z_val[:, LANES:]
        return z_val

    def conv_b(layer, idx, dst):
        left = jnp.concatenate([taps[q, 2 * idx + t] for q in range(3) for t in range(4)], axis=1)
        z_val = jnp.dot(left, wide_b[layer], preferred_element_type=F32)
        dst[2 * idx + 1, pl.ds(GUARD, block)] = z_val[:, :LANES]
        dst[2 * idx + 2, pl.ds(GUARD, block)] = z_val[:, LANES:]
        return z_val

    def add_sums(sums, z_val):
        tiles = z_val.reshape(block // 8, 8, 2 * LANES)
        return sums[0] + jnp.sum(tiles, axis=0), sums[1] + jnp.sum(tiles * tiles, axis=0)

    zero_sums = (jnp.zeros((8, 2 * LANES), F32), jnp.zeros((8, 2 * LANES), F32))

    def fold_sums(sums):
        rows_sum = [jnp.sum(val, axis=0, keepdims=True) for val in sums]
        return jnp.concatenate([val[:, :LANES] + val[:, LANES:] for val in rows_sum], axis=0)

    def sum_copy(layer, step):
        return pltpu.make_async_remote_copy(src_ref=parts.at[layer], dst_ref=slots.at[layer, me], send_sem=sum_send.at[layer],
                                            recv_sem=sum_recv.at[layer], device_id=peer_of(step), device_id_type=MESH_ID)

    def group_sum(layer, part):
        parts[layer] = part
        slots[layer, me] = part
        for step in range(1, total):
            sum_copy(layer, step).start()
        others = slots.at[layer, pl.ds(0, total - 1)]
        pltpu.make_async_copy(others, others, sum_recv.at[layer]).wait()
        return jnp.sum(slots[layer], axis=0)

    def finish_sum(layer):
        others = slots.at[layer, pl.ds(0, total - 1)]
        pltpu.make_async_copy(others, others, sum_send.at[layer]).wait()

    def scales(sums, count, gamma, beta):
        mean = sums[0:1] / count
        var = sums[1:2] / count - mean * mean
        return mean, gamma * lax.rsqrt(var + EPS_VALUE), beta

    def scales_a(sums, count, pair):
        both = sums + jnp.concatenate([sums[:, LANES // 2:], sums[:, :LANES // 2]], axis=1)
        twice = jnp.concatenate([pair, pair], axis=1)
        return scales(both, count, twice[0:1], twice[1:2])

    def normed(z_val, scale, keep=None):
        mean, gain, beta = scale
        if keep is not None:
            gain, beta = gain * keep, beta * keep
        return jnp.maximum((z_val - mean) * gain + beta, 0.0)

    keep_top = jnp.where(is_top, 0.0, 1.0).astype(F32)
    keep_bottom = jnp.where(is_bottom, 0.0, 1.0).astype(F32)
    lane = lax.broadcasted_iota(jnp.int32, (1, LANES), 1)
    upper_half = (lane < LANES // 2).astype(F32)
    lower_half = 1.0 - upper_half
    odd = pairs + 2

    for idx in range(n_chunk):
        image_copy(idx).wait()
    lax.fori_loop(2, pairs + 1, spread_pair, 0)
    sums = lax.fori_loop(2, pairs, lambda idx, acc: add_sums(acc, conv_a(0, idx)), zero_sums)

    @pl.when(jnp.logical_not(is_top))
    def _():
        image_down().wait_recv()

    @pl.when(jnp.logical_not(is_bottom))
    def _():
        image_up().wait_recv()

    lax.fori_loop(0, 2, spread_pair, 0)
    lax.fori_loop(pairs + 1, pairs + 3, spread_pair, 0)
    lax.fori_loop(0, 2, lambda idx, acc: (conv_a(0, idx * (pairs + 1)), acc)[1], 0)
    sums = lax.fori_loop(0, 2, lambda idx, acc: add_sums(acc, conv_a(0, 1 + idx * (pairs - 1))), sums)
    count_a = n_img * rows * width * total
    scale = scales_a(group_sum(0, fold_sums(sums)), count_a, norm_a[0])

    def taps_mid(scale, mid):
        def body(idx, carry):
            keep = mid(idx)
            taps[0, idx] = (normed(z_a[idx + odd, pl.ds(GUARD - 1, block)], scale, keep) * masks[0]).astype(BF16)
            taps[1, idx] = normed(z_a[idx, pl.ds(GUARD, block)], scale, keep).astype(BF16)
            taps[2, idx] = normed(z_a[idx + odd, pl.ds(GUARD, block)], scale, keep).astype(BF16)
            taps[3, idx] = (normed(z_a[idx, pl.ds(GUARD + 1, block)], scale, keep) * masks[1]).astype(BF16)
            return carry
        return body

    def keep_pairs(idx):
        return jnp.where(idx == 0, keep_top, jnp.where(idx == pairs + 1, keep_bottom, 1.0))

    lax.fori_loop(0, pairs + 2, taps_mid(scale, keep_pairs), 0)

    def sums_mid(idx, acc):
        z_val = conv_a(1, idx)
        own = jnp.where(idx == 0, lower_half, jnp.where(idx == pairs, upper_half, jnp.ones_like(lower_half)))
        own = jnp.concatenate([own, own], axis=1)
        new = add_sums(zero_sums, z_val)
        return acc[0] + own * new[0], acc[1] + own * new[1]

    sums = lax.fori_loop(0, pairs + 1, sums_mid, zero_sums)
    scale = scales_a(group_sum(1, fold_sums(sums)), count_a, norm_a[1])

    def keep_staggered(idx):
        return jnp.where(idx == pairs, upper_half + lower_half * keep_bottom, jnp.ones_like(lower_half))

    lax.fori_loop(0, pairs + 1, taps_mid(scale, keep_staggered), 0)
    sums = lax.fori_loop(0, pairs // 2, lambda idx, acc: add_sums(acc, conv_down(idx)), zero_sums)

    def edge_copies(ref, slot):
        below = pltpu.make_async_remote_copy(src_ref=ref.at[pairs], dst_ref=ref.at[0], send_sem=z_send.at[slot, 0], recv_sem=z_recv.at[slot, 0],
                                             device_id={'sp': sp_idx + 1}, device_id_type=MESH_ID)
        above = pltpu.make_async_remote_copy(src_ref=ref.at[1], dst_ref=ref.at[pairs + 1], send_sem=z_send.at[slot, 1], recv_sem=z_recv.at[slot, 1],
                                             device_id={'sp': sp_idx - 1}, device_id_type=MESH_ID)
        return below, above

    def send_edges(ref, slot):
        below, above = edge_copies(ref, slot)

        @pl.when(jnp.logical_not(is_bottom))
        def _():
            below.start()

        @pl.when(jnp.logical_not(is_top))
        def _():
            above.start()

    def recv_edges(ref, slot):
        below, above = edge_copies(ref, slot)

        @pl.when(jnp.logical_not(is_top))
        def _():
            below.wait_recv()

        @pl.when(jnp.logical_not(is_bottom))
        def _():
            above.wait_recv()

    def finish_edges(ref, slot):
        below, above = edge_copies(ref, slot)

        @pl.when(jnp.logical_not(is_bottom))
        def _():
            below.wait_send()

        @pl.when(jnp.logical_not(is_top))
        def _():
            above.wait_send()

    count_b = n_img * pairs * half * total
    send_edges(z_down, 0)
    sums_d = group_sum(2, fold_sums(sums))
    scale = scales(sums_d, count_b, norm_down[0:1], norm_down[1:2])
    recv_edges(z_down, 0)

    def taps_low(src, scale):
        def body(idx, carry):
            keep = jnp.where(idx == 0, keep_top, jnp.where(idx == pairs + 1, keep_bottom, 1.0))
            taps[0, idx] = (normed(src[idx, pl.ds(GUARD - 1, block)], scale, keep) * masks[0]).astype(BF16)
            taps[1, idx] = normed(src[idx, pl.ds(GUARD, block)], scale, keep).astype(BF16)
            taps[2, idx] = (normed(src[idx, pl.ds(GUARD + 1, block)], scale, keep) * masks[1]).astype(BF16)
            return carry
        return body

    lax.fori_loop(0, pairs + 2, taps_low(z_down, scale), 0)
    sums = lax.fori_loop(0, pairs // 2, lambda idx, acc: add_sums(acc, conv_b(0, idx, z_b)), zero_sums)
    send_edges(z_b, 1)
    sums_b = group_sum(3, fold_sums(sums))
    scale = scales(sums_b, count_b, norm_b[0, 0:1], norm_b[0, 1:2])
    recv_edges(z_b, 1)
    lax.fori_loop(0, pairs + 2, taps_low(z_b, scale), 0)
    sums = lax.fori_loop(0, pairs // 2, lambda idx, acc: add_sums(acc, conv_b(1, idx, z_last)), zero_sums)
    sums_b = group_sum(4, fold_sums(sums))
    scale = scales(sums_b, count_b, norm_b[1, 0:1], norm_b[1, 1:2])

    n_out = out_sems.shape[0]
    out_chunk = pairs // n_out

    def out_copy(idx):
        return pltpu.make_async_copy(out_rows.at[:, pl.ds(idx * out_chunk, out_chunk)], out.at[:, pl.ds(idx * out_chunk, out_chunk)], out_sems.at[idx])

    def out_body(row, carry):
        for img in range(n_img):
            out_rows[img, row] = normed(z_last[row + 1, pl.ds(GUARD + img * half, half)], scale).astype(BF16)
        return carry

    for idx in range(n_out):
        lax.fori_loop(idx * out_chunk, (idx + 1) * out_chunk, out_body, 0)
        out_copy(idx).start()

    @pl.when(jnp.logical_not(is_bottom))
    def _():
        image_down().wait_send()

    @pl.when(jnp.logical_not(is_top))
    def _():
        image_up().wait_send()

    finish_edges(z_down, 0)
    finish_edges(z_b, 1)
    for layer in range(5):
        finish_sum(layer)
    for idx in range(n_out):
        out_copy(idx).wait()


def solution(mesh):
    group_size = mesh.shape['sp']
    data_size = mesh.shape['dp']
    total = data_size * group_size

    def local_stack(images, w_a, norm_a, w_down, norm_down, w_b, norm_b):
        n_img, rows, width, ch_a = images.shape
        ch_b = w_down.shape[3]
        pairs, half = rows // 2, width // 2
        block = n_img * half
        padded = block + 2 * GUARD
        any_spec = pl.BlockSpec(memory_space=pl.ANY)
        vmem_spec = pl.BlockSpec(memory_space=pltpu.VMEM)
        n_chunk, n_out = 4, 4
        return pl.pallas_call(
            functools.partial(stack_kernel, data_size, group_size),
            out_shape=jax.ShapeDtypeStruct((n_img, pairs, half, ch_b), BF16),
            in_specs=[any_spec, any_spec, vmem_spec, any_spec, vmem_spec, any_spec, vmem_spec],
            out_specs=any_spec,
            scratch_shapes=[
                pltpu.VMEM((n_img, rows + 2 * HALO, width, ch_a), BF16),
                pltpu.VMEM(w_a.shape, BF16),
                pltpu.VMEM(w_down.shape, BF16),
                pltpu.VMEM(w_b.shape, BF16),
                pltpu.VMEM((2, 16 * ch_a, 2 * LANES), BF16),
                pltpu.VMEM((18 * ch_a, 2 * LANES), BF16),
                pltpu.VMEM((2, 12 * ch_b, 2 * LANES), BF16),
                pltpu.VMEM((n_img * width + 2 * GUARD, LANES), F32),
                pltpu.VMEM((2, block, LANES), F32),
                pltpu.VMEM((4, pairs + 3, block, LANES), BF16),
                pltpu.VMEM((2 * (pairs + 2), padded, LANES), F32),
                pltpu.VMEM((pairs + 2, padded, LANES), F32),
                pltpu.VMEM((pairs + 2, padded, LANES), F32),
                pltpu.VMEM((pairs + 2, padded, LANES), F32),
                pltpu.VMEM((n_img, pairs, half, ch_b), BF16),
                pltpu.VMEM((5, 2, LANES), F32),
                pltpu.VMEM((5, total, 2, LANES), F32),
                pltpu.SemaphoreType.DMA((n_chunk,)),
                pltpu.SemaphoreType.DMA((3,)),
                pltpu.SemaphoreType.DMA((n_out,)),
                pltpu.SemaphoreType.DMA((2,)),
                pltpu.SemaphoreType.DMA((2,)),
                pltpu.SemaphoreType.DMA((2, 2)),
                pltpu.SemaphoreType.DMA((2, 2)),
                pltpu.SemaphoreType.DMA((5,)),
                pltpu.SemaphoreType.DMA((5,)),
            ],
            compiler_params=pltpu.CompilerParams(collective_id=0, has_side_effects=True, vmem_limit_bytes=60 * 1024 * 1024),
            name='conv_stack',
        )(images, w_a, norm_a, w_down, norm_down, w_b, norm_b)

    act_spec = P(('pod', 'dp'), 'sp', None, None)
    return jax.shard_map(local_stack, mesh=mesh, in_specs=(act_spec, P(), P(), P(), P(), P(), P()), out_specs=act_spec, check_vma=False)
```

time: 370 us -> 76.7 us (0.21); the launches traced: 364 us -> 76.6 us
  blocking collectives: 224 us -> 0 us
  Pallas kernels: 0 us -> 73.5 us
  matrix products: 49 us -> 0 us
  other arithmetic: 31.1 us -> 0 us
  starting transfers between devices: 25.1 us -> 0 us
  waiting for transfers between devices: 22.3 us -> 0 us
  local copies, waits for them, and re-layouts: 12.4 us -> 3.03 us
    psum x5 -> x0, blocking collectives: 224 us -> none  [batch_norm(): group_sums = lax.psum(local_sums, ('dp', 'sp'))]
    pallas_call x0 -> x1, Pallas kernels: none -> 73.5 us  [local_stack(): pl.pallas_call(functools.partial(stack_kernel, data_size, group_size), ou...]
    conv_general_dilated x5 -> x0, matrix products: 49 us -> none  [the longest x4 41 us: same_layer(): lax.conv_general_dilated(padded, weight, (1, 1), ((0, 0), (1, 1)), dimens...]
    convert_element_type x5 -> x0, other arithmetic: 30.9 us -> none  [batch_norm(): return jnp.maximum(scaled, 0.0).astype(jnp.bfloat16)]
    ppermute x9 -> x0, starting transfers between devices: 25.1 us -> none  [the longest x4 13.1 us: same_layer(): top_rows = lax.ppermute(hidden[:, -1:], 'sp', to_lower)]
    ppermute x9 -> x0, waiting for transfers between devices: 22.3 us -> none  [the longest x4 16.7 us: same_layer(): bottom_rows = lax.ppermute(hidden[:, :1], 'sp', to_upper)]
    unnamed x13 -> x0, local copies, waits for them, and re-layouts: 8.3 us -> none
  transfers between devices with their start and end apart: 9 -> 0, of which waited for: 7 -> 0; matrix products, arithmetic and copies ran while one was open for 0% -> 0% of each run, Pallas kernels for 0% -> 0%
where the time goes in v1:
time: 76.7 us; the launch traced here: 76.6 us
  Pallas kernels  73.5 us (96%)
  local copies, waits for them, and re-layouts  3.03 us (4%)
    pallas_call x1, Pallas kernels, local_stack(): pl.pallas_call(functools.partial(stack_kernel, data_size, group_size), ou...  73.5 us
    pallas_call x1, local copies, waits for them, and re-layouts, local_stack(): pl.pallas_call(functools.partial(stack_kernel, data_size, group_size), ou...  3.03 us

profile of v1, /device:TPU:97, one launch (start us, length us, event | category | flops | bytes accessed | tf_op | source)
XLA Modules:
  0.0 76.6 jit_solution(1517585921674127184)
XLA Ops:
  0.0 73.5 %conv_stack.1 = bf16[12,16,28,128]{3,2,1,0:T(8,128)(2,1)} custom-call(bf16[12,32,56,64]{3,2,1,0:T(8,128)(2,1)} %images.1, bf16[2,3,3,64,64]{4,3,2,1,0:T(8,128)(2,1)} %w_a.1, f32[2,2,64]{2,1,0:T(2,128)} %norm_a.1, bf16[3,3,64,128]{3,2,1,0:T(8,128)(2,1)} %w_down.1, f32[2,128]{1,0:T(2,128)} %norm_down.1, bf16[2,3,3,128,128]{4,3,2,1,0:T(8,128)(2,1)} %w_b.1, ...), custom_call_target="tpu_custom_call" | custom-call | tf_op jit(solution)/shard_map/conv_stack/pallas_call | solution.py:385
  73.6 3.0 %copy.8 = bf16[12,16,28,128]{3,1,2,0:T(8,128)(2,1)} copy(bf16[12,16,28,128]{3,2,1,0:T(8,128)(2,1)} %conv_stack.1) | data formatting | bytes 2752512 | tf_op jit(solution)/shard_map/conv_stack/pallas_call | solution.py:385

commit v2 on v1

--- a/solution.py
+++ b/solution.py
@@ -17,10 +17,11 @@
 
 
 def stack_kernel(data_size, group_size, images, w_a, norm_a, w_down, norm_down, w_b, norm_b, out,
-                 x_in, w_a_in, w_down_in, w_b_in, wide_a, wide_down, wide_b, pixels, masks, taps, z_a, z_down, z_b, z_last,
+                 x_in, w_a_in, w_down_in, w_b_in, wide_a, wide_down, wide_b, pixels, masks, taps, z_a, z_mid, z_down, z_b, z_last,
                  out_rows, parts, slots, in_sems, w_sems, out_sems, image_send, image_recv, z_send, z_recv, sum_send, sum_recv):
     n_img, rows, width, _ = images.shape
     half = width // 2
+    last_stride = n_img * half + 1
     block = n_img * half
     pairs = rows // 2
     total = data_size * group_size
@@ -34,10 +35,6 @@
         other = lax.rem(me + step, total)
         return {'dp': other // group_size, 'sp': lax.rem(other, group_size)}
 
-    barrier = pltpu.get_barrier_semaphore()
-    for step in range(1, total):
-        pl.semaphore_signal(barrier, inc=1, device_id=peer_of(step), device_id_type=MESH_ID)
-
     n_chunk = in_sems.shape[0]
     chunk = rows // n_chunk
 
@@ -50,6 +47,10 @@
                      pltpu.make_async_copy(w_b, w_b_in, w_sems.at[2])]
     for copy in weight_copies:
         copy.start()
+
+    barrier = pltpu.get_barrier_semaphore()
+    for step in range(1, total):
+        pl.semaphore_signal(barrier, inc=1, device_id=peer_of(step), device_id_type=MESH_ID)
 
     pos = lax.rem(lax.broadcasted_iota(jnp.int32, (block, LANES), 0), half)
     masks[0] = (pos != 0).astype(F32)
@@ -66,6 +67,7 @@
         lax.fori_loop(0, outer, body, 0)
 
     clear_guards(z_a, z_a.shape[0])
+    clear_guards(z_mid, z_mid.shape[0])
 
     def clear_inner(ref):
         def body(idx, carry):
@@ -90,8 +92,6 @@
         z_down[pairs + 1] = jnp.zeros(z_down.shape[1:], F32)
         z_b[pairs + 1] = jnp.zeros(z_b.shape[1:], F32)
 
-    pl.semaphore_wait(barrier, total - 1)
-
     def image_down():
         return pltpu.make_async_remote_copy(src_ref=images.at[:, pl.ds(rows - HALO, HALO)], dst_ref=x_in.at[:, pl.ds(0, HALO)],
                                             send_sem=image_send.at[0], recv_sem=image_recv.at[0],
@@ -102,13 +102,14 @@
                                             send_sem=image_send.at[1], recv_sem=image_recv.at[1],
                                             device_id={'sp': sp_idx - 1}, device_id_type=MESH_ID)
 
-    @pl.when(jnp.logical_not(is_bottom))
-    def _():
-        image_down().start()
-
-    @pl.when(jnp.logical_not(is_top))
-    def _():
-        image_up().start()
+    def send_images():
+        @pl.when(jnp.logical_not(is_bottom))
+        def _():
+            image_down().start()
+
+        @pl.when(jnp.logical_not(is_top))
+        def _():
+            image_up().start()
 
     for copy in weight_copies:
         copy.wait()
@@ -138,7 +139,7 @@
                     p = t - d
                     wide_b[layer, pl.ds((q * 4 + t) * LANES, LANES), pl.ds(d * LANES, LANES)] = w_b_in[layer, p, q] if 0 <= p <= 2 else zero_b
 
-    def spread_pair(p, carry):
+    def spread_pair(p):
         upper = x_in[:, 2 * p].astype(F32)
         lower = x_in[:, 2 * p + 1].astype(F32)
         both = jnp.concatenate([upper, lower], axis=2)
@@ -147,13 +148,12 @@
         taps[1, p] = pixels[pl.ds(GUARD, block, stride=2)].astype(BF16)
         taps[2, p] = pixels[pl.ds(GUARD + 1, block, stride=2)].astype(BF16)
         taps[3, p] = (pixels[pl.ds(GUARD + 2, block, stride=2)] * masks[1]).astype(BF16)
-        return carry
-
-    def conv_a(layer, idx):
+
+    def conv_a(layer, idx, dst):
         left = jnp.concatenate([taps[q, idx + s] for q in range(4) for s in range(2)], axis=1)
         z_val = jnp.dot(left, wide_a[layer], preferred_element_type=F32)
-        z_a[idx, pl.ds(GUARD, block)] = z_val[:, :LANES]
-        z_a[idx + pairs + 2, pl.ds(GUARD, block)] = z_val[:, LANES:]
+        dst[idx, pl.ds(GUARD, block)] = z_val[:, :LANES]
+        dst[idx + dst.shape[0] // 2, pl.ds(GUARD, block)] = z_val[:, LANES:]
         return z_val
 
     def conv_down(idx):
@@ -163,12 +163,30 @@
         z_down[2 * idx + 2, pl.ds(GUARD, block)] = z_val[:, LANES:]
         return z_val
 
-    def conv_b(layer, idx, dst):
+    def conv_b(layer, idx):
         left = jnp.concatenate([taps[q, 2 * idx + t] for q in range(3) for t in range(4)], axis=1)
         z_val = jnp.dot(left, wide_b[layer], preferred_element_type=F32)
-        dst[2 * idx + 1, pl.ds(GUARD, block)] = z_val[:, :LANES]
-        dst[2 * idx + 2, pl.ds(GUARD, block)] = z_val[:, LANES:]
+        if layer == 0:
+            z_b[2 * idx + 1, pl.ds(GUARD, block)] = z_val[:, :LANES]
+            z_b[2 * idx + 2, pl.ds(GUARD, block)] = z_val[:, LANES:]
+        else:
+            z_last[pl.ds(2 * idx * last_stride, block)] = z_val[:, :LANES]
+            z_last[pl.ds((2 * idx + 1) * last_stride, block)] = z_val[:, LANES:]
         return z_val
+
+    def run(n_taps, first, per, n_conv, make_taps, conv, sums):
+        made = 0
+
+        def make_until(stop):
+            nonlocal made
+            while made < min(stop, n_taps):
+                make_taps(made)
+                made += 1
+
+        for idx in range(n_conv):
+            make_until(first + idx * per)
+            sums = conv(idx, sums)
+        return sums
 
     def add_sums(sums, z_val):
         tiles = z_val.reshape(block // 8, 8, 2 * LANES)
@@ -184,11 +202,13 @@
         return pltpu.make_async_remote_copy(src_ref=parts.at[layer], dst_ref=slots.at[layer, me], send_sem=sum_send.at[layer],
                                             recv_sem=sum_recv.at[layer], device_id=peer_of(step), device_id_type=MESH_ID)
 
-    def group_sum(layer, part):
+    def send_sums(layer, part):
         parts[layer] = part
         slots[layer, me] = part
         for step in range(1, total):
             sum_copy(layer, step).start()
+
+    def group_sum(layer):
         others = slots.at[layer, pl.ds(0, total - 1)]
         pltpu.make_async_copy(others, others, sum_recv.at[layer]).wait()
         return jnp.sum(slots[layer], axis=0)
@@ -218,12 +238,17 @@
     lane = lax.broadcasted_iota(jnp.int32, (1, LANES), 1)
     upper_half = (lane < LANES // 2).astype(F32)
     lower_half = 1.0 - upper_half
-    odd = pairs + 2
 
     for idx in range(n_chunk):
         image_copy(idx).wait()
-    lax.fori_loop(2, pairs + 1, spread_pair, 0)
-    sums = lax.fori_loop(2, pairs, lambda idx, acc: add_sums(acc, conv_a(0, idx)), zero_sums)
+
+    def conv_first(idx, acc):
+        if idx == 2:
+            pl.semaphore_wait(barrier, total - 1)
+            send_images()
+        return add_sums(acc, conv_a(0, 2 + idx, z_a))
+
+    sums = run(pairs - 1, 2, 1, pairs - 2, lambda idx: spread_pair(2 + idx), conv_first, zero_sums)
 
     @pl.when(jnp.logical_not(is_top))
     def _():
@@ -233,43 +258,46 @@
     def _():
         image_up().wait_recv()
 
-    lax.fori_loop(0, 2, spread_pair, 0)
-    lax.fori_loop(pairs + 1, pairs + 3, spread_pair, 0)
-    lax.fori_loop(0, 2, lambda idx, acc: (conv_a(0, idx * (pairs + 1)), acc)[1], 0)
-    sums = lax.fori_loop(0, 2, lambda idx, acc: add_sums(acc, conv_a(0, 1 + idx * (pairs - 1))), sums)
+    for idx in (0, 1, pairs + 1, pairs + 2):
+        spread_pair(idx)
+    for idx in (1, pairs):
+        sums = add_sums(sums, conv_a(0, idx, z_a))
+    send_sums(0, fold_sums(sums))
+    for idx in (0, pairs + 1):
+        conv_a(0, idx, z_a)
     count_a = n_img * rows * width * total
-    scale = scales_a(group_sum(0, fold_sums(sums)), count_a, norm_a[0])
-
-    def taps_mid(scale, mid):
-        def body(idx, carry):
-            keep = mid(idx)
-            taps[0, idx] = (normed(z_a[idx + odd, pl.ds(GUARD - 1, block)], scale, keep) * masks[0]).astype(BF16)
-            taps[1, idx] = normed(z_a[idx, pl.ds(GUARD, block)], scale, keep).astype(BF16)
-            taps[2, idx] = normed(z_a[idx + odd, pl.ds(GUARD, block)], scale, keep).astype(BF16)
-            taps[3, idx] = (normed(z_a[idx, pl.ds(GUARD + 1, block)], scale, keep) * masks[1]).astype(BF16)
-            return carry
-        return body
+    scale = scales_a(group_sum(0), count_a, norm_a[0])
+
+    def taps_mid(idx, src, scale, keep):
+        odd = idx + src.shape[0] // 2
+        taps[0, idx] = (normed(src[odd, pl.ds(GUARD - 1, block)], scale, keep) * masks[0]).astype(BF16)
+        taps[1, idx] = normed(src[idx, pl.ds(GUARD, block)], scale, keep).astype(BF16)
+        taps[2, idx] = normed(src[odd, pl.ds(GUARD, block)], scale, keep).astype(BF16)
+        taps[3, idx] = (normed(src[idx, pl.ds(GUARD + 1, block)], scale, keep) * masks[1]).astype(BF16)
 
     def keep_pairs(idx):
-        return jnp.where(idx == 0, keep_top, jnp.where(idx == pairs + 1, keep_bottom, 1.0))
-
-    lax.fori_loop(0, pairs + 2, taps_mid(scale, keep_pairs), 0)
-
-    def sums_mid(idx, acc):
-        z_val = conv_a(1, idx)
-        own = jnp.where(idx == 0, lower_half, jnp.where(idx == pairs, upper_half, jnp.ones_like(lower_half)))
-        own = jnp.concatenate([own, own], axis=1)
-        new = add_sums(zero_sums, z_val)
-        return acc[0] + own * new[0], acc[1] + own * new[1]
-
-    sums = lax.fori_loop(0, pairs + 1, sums_mid, zero_sums)
-    scale = scales_a(group_sum(1, fold_sums(sums)), count_a, norm_a[1])
+        return keep_top if idx == 0 else keep_bottom if idx == pairs + 1 else None
+
+    def conv_second(idx, acc):
+        z_val = conv_a(1, idx, z_mid)
+        if idx in (0, pairs):
+            own = lower_half if idx == 0 else upper_half
+            own = jnp.concatenate([own, own], axis=1)
+            new = add_sums(zero_sums, z_val)
+            return acc[0] + own * new[0], acc[1] + own * new[1]
+        return add_sums(acc, z_val)
+
+    sums = run(pairs + 2, 2, 1, pairs + 1, lambda idx: taps_mid(idx, z_a, scale, keep_pairs(idx)), conv_second, zero_sums)
+    send_sums(1, fold_sums(sums))
+    scale_mid = scales_a(group_sum(1), count_a, norm_a[1])
 
     def keep_staggered(idx):
-        return jnp.where(idx == pairs, upper_half + lower_half * keep_bottom, jnp.ones_like(lower_half))
-
-    lax.fori_loop(0, pairs + 1, taps_mid(scale, keep_staggered), 0)
-    sums = lax.fori_loop(0, pairs // 2, lambda idx, acc: add_sums(acc, conv_down(idx)), zero_sums)
+        return upper_half + lower_half * keep_bottom if idx == pairs else None
+
+    def conv_third(idx, acc):
+        return add_sums(acc, conv_down(idx))
+
+    sums = run(pairs + 1, 3, 2, pairs // 2, lambda idx: taps_mid(idx, z_mid, scale_mid, keep_staggered(idx)), conv_third, zero_sums)
 
     def edge_copies(ref, slot):
         below = pltpu.make_async_remote_copy(src_ref=ref.at[pairs], dst_ref=ref.at[0], send_sem=z_send.at[slot, 0], recv_sem=z_recv.at[slot, 0],
@@ -312,40 +340,42 @@
             above.wait_send()
 
     count_b = n_img * pairs * half * total
+    send_sums(2, fold_sums(sums))
     send_edges(z_down, 0)
-    sums_d = group_sum(2, fold_sums(sums))
-    scale = scales(sums_d, count_b, norm_down[0:1], norm_down[1:2])
+    scale_down = scales(group_sum(2), count_b, norm_down[0:1], norm_down[1:2])
     recv_edges(z_down, 0)
 
-    def taps_low(src, scale):
-        def body(idx, carry):
-            keep = jnp.where(idx == 0, keep_top, jnp.where(idx == pairs + 1, keep_bottom, 1.0))
-            taps[0, idx] = (normed(src[idx, pl.ds(GUARD - 1, block)], scale, keep) * masks[0]).astype(BF16)
-            taps[1, idx] = normed(src[idx, pl.ds(GUARD, block)], scale, keep).astype(BF16)
-            taps[2, idx] = (normed(src[idx, pl.ds(GUARD + 1, block)], scale, keep) * masks[1]).astype(BF16)
-            return carry
-        return body
-
-    lax.fori_loop(0, pairs + 2, taps_low(z_down, scale), 0)
-    sums = lax.fori_loop(0, pairs // 2, lambda idx, acc: add_sums(acc, conv_b(0, idx, z_b)), zero_sums)
+    def taps_low(idx, src, scale):
+        keep = keep_pairs(idx)
+        taps[0, idx] = (normed(src[idx, pl.ds(GUARD - 1, block)], scale, keep) * masks[0]).astype(BF16)
+        taps[1, idx] = normed(src[idx, pl.ds(GUARD, block)], scale, keep).astype(BF16)
+        taps[2, idx] = (normed(src[idx, pl.ds(GUARD + 1, block)], scale, keep) * masks[1]).astype(BF16)
+
+    def conv_fourth(idx, acc):
+        return add_sums(acc, conv_b(0, idx))
+
+    def conv_fifth(idx, acc):
+        return add_sums(acc, conv_b(1, idx))
+
+    sums = run(pairs + 2, 4, 2, pairs // 2, lambda idx: taps_low(idx, z_down, scale_down), conv_fourth, zero_sums)
+    send_sums(3, fold_sums(sums))
     send_edges(z_b, 1)
-    sums_b = group_sum(3, fold_sums(sums))
-    scale = scales(sums_b, count_b, norm_b[0, 0:1], norm_b[0, 1:2])
+    scale_b = scales(group_sum(3), count_b, norm_b[0, 0:1], norm_b[0, 1:2])
     recv_edges(z_b, 1)
-    lax.fori_loop(0, pairs + 2, taps_low(z_b, scale), 0)
-    sums = lax.fori_loop(0, pairs // 2, lambda idx, acc: add_sums(acc, conv_b(1, idx, z_last)), zero_sums)
-    sums_b = group_sum(4, fold_sums(sums))
-    scale = scales(sums_b, count_b, norm_b[1, 0:1], norm_b[1, 1:2])
+    sums = run(pairs + 2, 4, 2, pairs // 2, lambda idx: taps_low(idx, z_b, scale_b), conv_fifth, zero_sums)
+    send_sums(4, fold_sums(sums))
+    scale = scales(group_sum(4), count_b, norm_b[1, 0:1], norm_b[1, 1:2])
 
     n_out = out_sems.shape[0]
-    out_chunk = pairs // n_out
+    out_chunk = n_img // n_out
 
     def out_copy(idx):
-        return pltpu.make_async_copy(out_rows.at[:, pl.ds(idx * out_chunk, out_chunk)], out.at[:, pl.ds(idx * out_chunk, out_chunk)], out_sems.at[idx])
-
-    def out_body(row, carry):
-        for img in range(n_img):
-            out_rows[img, row] = normed(z_last[row + 1, pl.ds(GUARD + img * half, half)], scale).astype(BF16)
+        return pltpu.make_async_copy(out_rows.at[pl.ds(idx * out_chunk, out_chunk)], out.at[pl.ds(idx * out_chunk, out_chunk)], out_sems.at[idx])
+
+    def out_body(img, carry):
+        for col in range(half):
+            rows_val = z_last[pl.ds(img * half + col, pairs, stride=last_stride)]
+            out_rows[img, col] = normed(rows_val, scale).astype(BF16)
         return carry
 
     for idx in range(n_out):
@@ -382,9 +412,9 @@
         any_spec = pl.BlockSpec(memory_space=pl.ANY)
         vmem_spec = pl.BlockSpec(memory_space=pltpu.VMEM)
         n_chunk, n_out = 4, 4
-        return pl.pallas_call(
+        result = pl.pallas_call(
             functools.partial(stack_kernel, data_size, group_size),
-            out_shape=jax.ShapeDtypeStruct((n_img, pairs, half, ch_b), BF16),
+            out_shape=jax.ShapeDtypeStruct((n_img, half, pairs, ch_b), BF16),
             in_specs=[any_spec, any_spec, vmem_spec, any_spec, vmem_spec, any_spec, vmem_spec],
             out_specs=any_spec,
             scratch_shapes=[
@@ -399,10 +429,11 @@
                 pltpu.VMEM((2, block, LANES), F32),
                 pltpu.VMEM((4, pairs + 3, block, LANES), BF16),
                 pltpu.VMEM((2 * (pairs + 2), padded, LANES), F32),
+                pltpu.VMEM((2 * (pairs + 1), padded, LANES), F32),
                 pltpu.VMEM((pairs + 2, padded, LANES), F32),
                 pltpu.VMEM((pairs + 2, padded, LANES), F32),
-                pltpu.VMEM((pairs + 2, padded, LANES), F32),
-                pltpu.VMEM((n_img, pairs, half, ch_b), BF16),
+                pltpu.VMEM((pairs * (block + 1) + 7, LANES), F32),
+                pltpu.VMEM((n_img, half, pairs, ch_b), BF16),
                 pltpu.VMEM((5, 2, LANES), F32),
                 pltpu.VMEM((5, total, 2, LANES), F32),
                 pltpu.SemaphoreType.DMA((n_chunk,)),
@@ -418,6 +449,7 @@
             compiler_params=pltpu.CompilerParams(collective_id=0, has_side_effects=True, vmem_limit_bytes=60 * 1024 * 1024),
             name='conv_stack',
         )(images, w_a, norm_a, w_down, norm_down, w_b, norm_b)
+        return jnp.transpose(result, (0, 2, 1, 3))
 
     act_spec = P(('pod', 'dp'), 'sp', None, None)
     return jax.shard_map(local_stack, mesh=mesh, in_specs=(act_spec, P(), P(), P(), P(), P(), P()), out_specs=act_spec, check_vma=False)

time: 76.7 us -> 59.2 us (0.77)
  Pallas kernels: 73.5 us -> 56.4 us
    pallas_call x1, Pallas kernels: 73.5 us -> 56.4 us  [local_stack(): pl.pallas_call(functools.partial(stack_kernel, data_size, group_size), ou...]
    pallas_call x1 -> x0, local copies, waits for them, and re-layouts: 3.03 us -> none  [local_stack(): pl.pallas_call(functools.partial(stack_kernel, data_size, group_size), ou...]
    unnamed x0 -> x1, local copies, waits for them, and re-layouts: none -> 2.65 us
where the time goes in v2:
time: 59.2 us; the launch traced here: 59.1 us
  Pallas kernels  56.4 us (95%)
  local copies, waits for them, and re-layouts  2.65 us (4%)
    pallas_call x1, Pallas kernels, local_stack(): pl.pallas_call(functools.partial(stack_kernel, data_size, group_size), ou...  56.4 us
    unnamed x1, local copies, waits for them, and re-layouts  2.65 us

profile of v2, /device:TPU:97, one launch (start us, length us, event | category | flops | bytes accessed | tf_op | source)
XLA Modules:
  0.0 59.1 jit_solution(2403529362705572551)
XLA Ops:
  0.0 56.4 %conv_stack.1 = bf16[12,28,16,128]{3,2,1,0:T(8,128)(2,1)} custom-call(bf16[12,32,56,64]{3,2,1,0:T(8,128)(2,1)} %images.1, bf16[2,3,3,64,64]{4,3,2,1,0:T(8,128)(2,1)} %w_a.1, f32[2,2,64]{2,1,0:T(2,128)} %norm_a.1, bf16[3,3,64,128]{3,2,1,0:T(8,128)(2,1)} %w_down.1, f32[2,128]{1,0:T(2,128)} %norm_down.1, bf16[2,3,3,128,128]{4,3,2,1,0:T(8,128)(2,1)} %w_b.1, ...), custom_call_target="tpu_custom_call" | custom-call | tf_op jit(solution)/shard_map/conv_stack/pallas_call | solution.py:415
  56.4 2.7 %copy.9 = bf16[12,16,28,128]{3,1,2,0:T(8,128)(2,1)} copy(bf16[12,16,28,128]{3,1,2,0:T(8,128)(2,1)} %bitcast.1) | data formatting | bytes 2752512

commit v3 on v2

--- a/solution.py
+++ b/solution.py
@@ -10,15 +10,15 @@
 EPS_VALUE = 1e-5
 MESH_ID = pl.DeviceIdType.MESH
 LANES = 128
-HALO = 3
 GUARD = 8
 F32 = jnp.float32
 BF16 = jnp.bfloat16
 
 
-def stack_kernel(data_size, group_size, images, w_a, norm_a, w_down, norm_down, w_b, norm_b, out,
-                 x_in, w_a_in, w_down_in, w_b_in, wide_a, wide_down, wide_b, pixels, masks, taps, z_a, z_mid, z_down, z_b, z_last,
-                 out_rows, parts, slots, in_sems, w_sems, out_sems, image_send, image_recv, z_send, z_recv, sum_send, sum_recv):
+def stack_kernel(data_size, group_size, images, w_a, norm_a, w_down, norm_down, w_b, norm_b, z_out, mean_out, gain_out, beta_out,
+                 x_in, w_a_in, w_down_in, w_b_in, norm_a_in, norm_down_in, norm_b_in, wide_a, wide_down, wide_b,
+                 send_low, send_up, from_up, from_low, pixels, masks, taps, z_a, z_mid, z_down, z_b, z_last, z_turned, scale_rows,
+                 parts, slots, in_sems, w_sems, out_sems, image_send, image_recv, z_send, z_recv, sum_send, sum_recv):
     n_img, rows, width, _ = images.shape
     half = width // 2
     last_stride = n_img * half + 1
@@ -31,26 +31,35 @@
     is_top = sp_idx == 0
     is_bottom = sp_idx == group_size - 1
 
-    def peer_of(step):
-        other = lax.rem(me + step, total)
-        return {'dp': other // group_size, 'sp': lax.rem(other, group_size)}
+    ring = group_size // 2
+
+    def distance(peer):
+        return min(peer[0], data_size - peer[0]) + min(peer[1], ring - peer[1])
+
+    offsets = [(d, x, c) for d in range(data_size) for x in range(ring) for c in range(2)][1:]
+    offsets.sort(key=distance, reverse=True)
+
+    def peer_of(offset):
+        core = lax.rem(sp_idx, 2)
+        place = lax.rem(sp_idx // 2 + offset[1], ring)
+        return {'dp': lax.rem(dp_idx + offset[0], data_size), 'sp': place * 2 + (1 - core if offset[2] else core)}
 
     n_chunk = in_sems.shape[0]
     chunk = rows // n_chunk
 
     def image_copy(idx):
-        return pltpu.make_async_copy(images.at[:, pl.ds(idx * chunk, chunk)], x_in.at[:, pl.ds(HALO + idx * chunk, chunk)], in_sems.at[idx])
-
-    for idx in range(n_chunk):
+        return pltpu.make_async_copy(images.at[:, pl.ds(idx * chunk, chunk)], x_in.at[:, pl.ds(idx * chunk, chunk)], in_sems.at[idx])
+
+    for idx in [0, n_chunk - 1] + list(range(1, n_chunk - 1)):
         image_copy(idx).start()
-    weight_copies = [pltpu.make_async_copy(w_a, w_a_in, w_sems.at[0]), pltpu.make_async_copy(w_down, w_down_in, w_sems.at[1]),
-                     pltpu.make_async_copy(w_b, w_b_in, w_sems.at[2])]
-    for copy in weight_copies:
+    small_pairs = [(w_a, w_a_in), (norm_a, norm_a_in), (w_down, w_down_in), (norm_down, norm_down_in), (w_b, w_b_in), (norm_b, norm_b_in)]
+    small_copies = [pltpu.make_async_copy(src, dst, w_sems.at[idx]) for idx, (src, dst) in enumerate(small_pairs)]
+    for copy in small_copies:
         copy.start()
 
     barrier = pltpu.get_barrier_semaphore()
-    for step in range(1, total):
-        pl.semaphore_signal(barrier, inc=1, device_id=peer_of(step), device_id_type=MESH_ID)
+    for offset in offsets:
+        pl.semaphore_signal(barrier, inc=1, device_id=peer_of(offset), device_id_type=MESH_ID)
 
     pos = lax.rem(lax.broadcasted_iota(jnp.int32, (block, LANES), 0), half)
     masks[0] = (pos != 0).astype(F32)
@@ -66,8 +75,6 @@
             return carry
         lax.fori_loop(0, outer, body, 0)
 
-    clear_guards(z_a, z_a.shape[0])
-    clear_guards(z_mid, z_mid.shape[0])
 
     def clear_inner(ref):
         def body(idx, carry):
@@ -77,29 +84,44 @@
             return carry
         lax.fori_loop(1, pairs + 1, body, 0)
 
-    clear_inner(z_down)
-    clear_inner(z_b)
-
     @pl.when(is_top)
     def _():
-        x_in[:, 0:HALO] = jnp.zeros((n_img, HALO, width, x_in.shape[3]), BF16)
+        from_up[...] = jnp.zeros(from_up.shape, BF16)
         z_down[0] = jnp.zeros(z_down.shape[1:], F32)
         z_b[0] = jnp.zeros(z_b.shape[1:], F32)
 
     @pl.when(is_bottom)
     def _():
-        x_in[:, HALO + rows:] = jnp.zeros((n_img, HALO, width, x_in.shape[3]), BF16)
+        from_low[...] = jnp.zeros(from_low.shape, BF16)
         z_down[pairs + 1] = jnp.zeros(z_down.shape[1:], F32)
         z_b[pairs + 1] = jnp.zeros(z_b.shape[1:], F32)
 
+    waited = set()
+
+    def need_row(row):
+        idx = row // chunk
+        if idx not in waited:
+            waited.add(idx)
+            image_copy(idx).wait()
+
+    for row in (0, rows - 1):
+        need_row(row)
+    plane = n_img * width
+
+    def two_rows(row):
+        return jnp.concatenate([x_in[:, row].astype(F32), x_in[:, row + 1].astype(F32)], axis=2).reshape(plane, LANES).astype(BF16)
+
+    send_low[...] = two_rows(rows - 2)
+    send_up[pl.ds(0, plane)] = two_rows(0)
+    third = [x_in[pl.ds(idx * (n_img // 2), n_img // 2), 2].astype(F32) for idx in range(2)]
+    send_up[pl.ds(plane, plane // 2)] = jnp.concatenate(third, axis=2).reshape(plane // 2, LANES).astype(BF16)
+
     def image_down():
-        return pltpu.make_async_remote_copy(src_ref=images.at[:, pl.ds(rows - HALO, HALO)], dst_ref=x_in.at[:, pl.ds(0, HALO)],
-                                            send_sem=image_send.at[0], recv_sem=image_recv.at[0],
+        return pltpu.make_async_remote_copy(src_ref=send_low, dst_ref=from_up, send_sem=image_send.at[0], recv_sem=image_recv.at[0],
                                             device_id={'sp': sp_idx + 1}, device_id_type=MESH_ID)
 
     def image_up():
-        return pltpu.make_async_remote_copy(src_ref=images.at[:, pl.ds(0, HALO)], dst_ref=x_in.at[:, pl.ds(HALO + rows, HALO)],
-                                            send_sem=image_send.at[1], recv_sem=image_recv.at[1],
+        return pltpu.make_async_remote_copy(src_ref=send_up, dst_ref=from_low, send_sem=image_send.at[1], recv_sem=image_recv.at[1],
                                             device_id={'sp': sp_idx - 1}, device_id_type=MESH_ID)
 
     def send_images():
@@ -111,8 +133,6 @@
         def _():
             image_up().start()
 
-    for copy in weight_copies:
-        copy.wait()
     ch_a = w_a.shape[3]
     zero_a = jnp.zeros((ch_a, ch_a), BF16)
     zero_b = jnp.zeros((LANES, LANES), BF16)
@@ -121,29 +141,45 @@
     def tap_a(layer, p, q):
         return w_a_in[layer, p, q] if 0 <= p <= 2 and 0 <= q <= 2 else zero_a
 
-    for layer in range(2):
+    def widen_a(layer):
         for q in range(4):
             for t in range(4):
                 for dw in range(2):
                     both = jnp.concatenate([tap_a(layer, t, q - dw), tap_a(layer, t - 1, q - dw)], axis=1)
                     wide_a[layer, pl.ds((q * 4 + t) * ch_a, ch_a), pl.ds(dw * LANES, LANES)] = both
-    for q in range(3):
-        for t in range(6):
-            for d in range(2):
-                p = t - 1 - 2 * d
-                wide_down[pl.ds((q * 6 + t) * ch_a, ch_a), pl.ds(d * LANES, LANES)] = w_down_in[p, q] if 0 <= p <= 2 else zero_d
-    for layer in range(2):
+
+    def widen_down():
         for q in range(3):
-            for t in range(4):
+            for t in range(6):
                 for d in range(2):
-                    p = t - d
-                    wide_b[layer, pl.ds((q * 4 + t) * LANES, LANES), pl.ds(d * LANES, LANES)] = w_b_in[layer, p, q] if 0 <= p <= 2 else zero_b
+                    p = t - 1 - 2 * d
+                    wide_down[pl.ds((q * 6 + t) * ch_a, ch_a), pl.ds(d * LANES, LANES)] = w_down_in[p, q] if 0 <= p <= 2 else zero_d
+
+    def widen_b():
+        for layer in range(2):
+            for q in range(3):
+                for t in range(4):
+                    for d in range(2):
+                        p = t - d
+                        wide_b[layer, pl.ds((q * 4 + t) * LANES, LANES), pl.ds(d * LANES, LANES)] = w_b_in[layer, p, q] if 0 <= p <= 2 else zero_b
+
+    def image_row(row):
+        half_a = LANES // 2
+        if row < -2:
+            return jnp.zeros((plane, half_a), F32)
+        if row < 0:
+            return from_up[:, (row + 2) * half_a:(row + 3) * half_a].astype(F32)
+        if row < rows:
+            need_row(row)
+            return x_in[:, row].astype(F32).reshape(plane, half_a)
+        if row < rows + 2:
+            return from_low[pl.ds(0, plane), (row - rows) * half_a:(row - rows + 1) * half_a].astype(F32)
+        packed = from_low[pl.ds(plane, plane // 2), :].astype(F32)
+        return jnp.concatenate([packed[:, :half_a], packed[:, half_a:]], axis=0)
 
     def spread_pair(p):
-        upper = x_in[:, 2 * p].astype(F32)
-        lower = x_in[:, 2 * p + 1].astype(F32)
-        both = jnp.concatenate([upper, lower], axis=2)
-        pixels[pl.ds(GUARD, n_img * width)] = both.reshape(n_img * width, LANES)
+        both = jnp.concatenate([image_row(2 * p - 3), image_row(2 * p - 2)], axis=1)
+        pixels[pl.ds(GUARD, n_img * width)] = both
         taps[0, p] = (pixels[pl.ds(GUARD - 1, block, stride=2)] * masks[0]).astype(BF16)
         taps[1, p] = pixels[pl.ds(GUARD, block, stride=2)].astype(BF16)
         taps[2, p] = pixels[pl.ds(GUARD + 1, block, stride=2)].astype(BF16)
@@ -198,15 +234,15 @@
         rows_sum = [jnp.sum(val, axis=0, keepdims=True) for val in sums]
         return jnp.concatenate([val[:, :LANES] + val[:, LANES:] for val in rows_sum], axis=0)
 
-    def sum_copy(layer, step):
+    def sum_copy(layer, offset):
         return pltpu.make_async_remote_copy(src_ref=parts.at[layer], dst_ref=slots.at[layer, me], send_sem=sum_send.at[layer],
-                                            recv_sem=sum_recv.at[layer], device_id=peer_of(step), device_id_type=MESH_ID)
+                                            recv_sem=sum_recv.at[layer], device_id=peer_of(offset), device_id_type=MESH_ID)
 
     def send_sums(layer, part):
         parts[layer] = part
         slots[layer, me] = part
-        for step in range(1, total):
-            sum_copy(layer, step).start()
+        for offset in offsets:
+            sum_copy(layer, offset).start()
 
     def group_sum(layer):
         others = slots.at[layer, pl.ds(0, total - 1)]
@@ -239,11 +275,11 @@
     upper_half = (lane < LANES // 2).astype(F32)
     lower_half = 1.0 - upper_half
 
-    for idx in range(n_chunk):
-        image_copy(idx).wait()
+    small_copies[0].wait()
+    widen_a(0)
 
     def conv_first(idx, acc):
-        if idx == 2:
+        if idx == 1:
             pl.semaphore_wait(barrier, total - 1)
             send_images()
         return add_sums(acc, conv_a(0, 2 + idx, z_a))
@@ -254,23 +290,36 @@
     def _():
         image_down().wait_recv()
 
+    spread_pair(1)
+    sums = add_sums(sums, conv_a(0, 1, z_a))
+
     @pl.when(jnp.logical_not(is_bottom))
     def _():
         image_up().wait_recv()
 
-    for idx in (0, 1, pairs + 1, pairs + 2):
-        spread_pair(idx)
-    for idx in (1, pairs):
-        sums = add_sums(sums, conv_a(0, idx, z_a))
+    spread_pair(pairs + 1)
+    sums = add_sums(sums, conv_a(0, pairs, z_a))
     send_sums(0, fold_sums(sums))
-    for idx in (0, pairs + 1):
-        conv_a(0, idx, z_a)
+    spread_pair(0)
+    conv_a(0, 0, z_a)
+    spread_pair(pairs + 2)
+    conv_a(0, pairs + 1, z_a)
+    for copy in small_copies[1:]:
+        copy.wait()
+    widen_a(1)
+    widen_down()
+    widen_b()
+    clear_guards(z_a, z_a.shape[0])
+    clear_guards(z_mid, z_mid.shape[0])
+    clear_inner(z_down)
+    clear_inner(z_b)
     count_a = n_img * rows * width * total
-    scale = scales_a(group_sum(0), count_a, norm_a[0])
-
-    def taps_mid(idx, src, scale, keep):
+    scale = scales_a(group_sum(0), count_a, norm_a_in[0])
+
+    def taps_mid(idx, src, scale, keep, left=True):
         odd = idx + src.shape[0] // 2
-        taps[0, idx] = (normed(src[odd, pl.ds(GUARD - 1, block)], scale, keep) * masks[0]).astype(BF16)
+        if left:
+            taps[0, idx] = (normed(src[odd, pl.ds(GUARD - 1, block)], scale, keep) * masks[0]).astype(BF16)
         taps[1, idx] = normed(src[idx, pl.ds(GUARD, block)], scale, keep).astype(BF16)
         taps[2, idx] = normed(src[odd, pl.ds(GUARD, block)], scale, keep).astype(BF16)
         taps[3, idx] = (normed(src[idx, pl.ds(GUARD + 1, block)], scale, keep) * masks[1]).astype(BF16)
@@ -289,7 +338,7 @@
 
     sums = run(pairs + 2, 2, 1, pairs + 1, lambda idx: taps_mid(idx, z_a, scale, keep_pairs(idx)), conv_second, zero_sums)
     send_sums(1, fold_sums(sums))
-    scale_mid = scales_a(group_sum(1), count_a, norm_a[1])
+    scale_mid = scales_a(group_sum(1), count_a, norm_a_in[1])
 
     def keep_staggered(idx):
         return upper_half + lower_half * keep_bottom if idx == pairs else None
@@ -297,7 +346,7 @@
     def conv_third(idx, acc):
         return add_sums(acc, conv_down(idx))
 
-    sums = run(pairs + 1, 3, 2, pairs // 2, lambda idx: taps_mid(idx, z_mid, scale_mid, keep_staggered(idx)), conv_third, zero_sums)
+    sums = run(pairs + 1, 3, 2, pairs // 2, lambda idx: taps_mid(idx, z_mid, scale_mid, keep_staggered(idx), left=False), conv_third, zero_sums)
 
     def edge_copies(ref, slot):
         below = pltpu.make_async_remote_copy(src_ref=ref.at[pairs], dst_ref=ref.at[0], send_sem=z_send.at[slot, 0], recv_sem=z_recv.at[slot, 0],
@@ -342,7 +391,7 @@
     count_b = n_img * pairs * half * total
     send_sums(2, fold_sums(sums))
     send_edges(z_down, 0)
-    scale_down = scales(group_sum(2), count_b, norm_down[0:1], norm_down[1:2])
+    scale_down = scales(group_sum(2), count_b, norm_down_in[0:1], norm_down_in[1:2])
     recv_edges(z_down, 0)
 
     def taps_low(idx, src, scale):
@@ -360,27 +409,33 @@
     sums = run(pairs + 2, 4, 2, pairs // 2, lambda idx: taps_low(idx, z_down, scale_down), conv_fourth, zero_sums)
     send_sums(3, fold_sums(sums))
     send_edges(z_b, 1)
-    scale_b = scales(group_sum(3), count_b, norm_b[0, 0:1], norm_b[0, 1:2])
+    scale_b = scales(group_sum(3), count_b, norm_b_in[0, 0:1], norm_b_in[0, 1:2])
     recv_edges(z_b, 1)
     sums = run(pairs + 2, 4, 2, pairs // 2, lambda idx: taps_low(idx, z_b, scale_b), conv_fifth, zero_sums)
     send_sums(4, fold_sums(sums))
-    scale = scales(group_sum(4), count_b, norm_b[1, 0:1], norm_b[1, 1:2])
-
-    n_out = out_sems.shape[0]
+
+    n_out = out_sems.shape[0] - 3
     out_chunk = n_img // n_out
 
     def out_copy(idx):
-        return pltpu.make_async_copy(out_rows.at[pl.ds(idx * out_chunk, out_chunk)], out.at[pl.ds(idx * out_chunk, out_chunk)], out_sems.at[idx])
-
-    def out_body(img, carry):
+        part = pl.ds(idx * out_chunk, out_chunk)
+        return pltpu.make_async_copy(z_turned.at[part], z_out.at[part], out_sems.at[idx])
+
+    def turn(img, carry):
         for col in range(half):
-            rows_val = z_last[pl.ds(img * half + col, pairs, stride=last_stride)]
-            out_rows[img, col] = normed(rows_val, scale).astype(BF16)
+            z_turned[img, col] = z_last[pl.ds(img * half + col, pairs, stride=last_stride)]
         return carry
 
     for idx in range(n_out):
-        lax.fori_loop(idx * out_chunk, (idx + 1) * out_chunk, out_body, 0)
+        lax.fori_loop(idx * out_chunk, (idx + 1) * out_chunk, turn, 0)
         out_copy(idx).start()
+    mean, gain, beta = scales(group_sum(4), count_b, norm_b_in[1, 0:1], norm_b_in[1, 1:2])
+    scale_copies = []
+    for idx, (val, dst) in enumerate([(mean, mean_out), (gain, gain_out), (beta, beta_out)]):
+        scale_rows[idx] = val
+        scale_copies.append(pltpu.make_async_copy(scale_rows.at[idx], dst, out_sems.at[n_out + idx]))
+    for copy in scale_copies:
+        copy.start()
 
     @pl.when(jnp.logical_not(is_bottom))
     def _():
@@ -396,6 +451,8 @@
         finish_sum(layer)
     for idx in range(n_out):
         out_copy(idx).wait()
+    for copy in scale_copies:
+        copy.wait()
 
 
 def solution(mesh):
@@ -410,21 +467,27 @@
         block = n_img * half
         padded = block + 2 * GUARD
         any_spec = pl.BlockSpec(memory_space=pl.ANY)
-        vmem_spec = pl.BlockSpec(memory_space=pltpu.VMEM)
-        n_chunk, n_out = 4, 4
-        result = pl.pallas_call(
+        n_chunk, n_out = 8, 4
+        z_val, mean, gain, beta = pl.pallas_call(
             functools.partial(stack_kernel, data_size, group_size),
-            out_shape=jax.ShapeDtypeStruct((n_img, half, pairs, ch_b), BF16),
-            in_specs=[any_spec, any_spec, vmem_spec, any_spec, vmem_spec, any_spec, vmem_spec],
-            out_specs=any_spec,
+            out_shape=(jax.ShapeDtypeStruct((n_img, half, pairs, ch_b), F32),) + (jax.ShapeDtypeStruct((1, LANES), F32),) * 3,
+            in_specs=[any_spec] * 7,
+            out_specs=(any_spec,) * 4,
             scratch_shapes=[
-                pltpu.VMEM((n_img, rows + 2 * HALO, width, ch_a), BF16),
+                pltpu.VMEM((n_img, rows, width, ch_a), BF16),
                 pltpu.VMEM(w_a.shape, BF16),
                 pltpu.VMEM(w_down.shape, BF16),
                 pltpu.VMEM(w_b.shape, BF16),
+                pltpu.VMEM(norm_a.shape, F32),
+                pltpu.VMEM(norm_down.shape, F32),
+                pltpu.VMEM(norm_b.shape, F32),
                 pltpu.VMEM((2, 16 * ch_a, 2 * LANES), BF16),
                 pltpu.VMEM((18 * ch_a, 2 * LANES), BF16),
                 pltpu.VMEM((2, 12 * ch_b, 2 * LANES), BF16),
+                pltpu.VMEM((n_img * width, LANES), BF16),
+                pltpu.VMEM((n_img * width * 3 // 2, LANES), BF16),
+                pltpu.VMEM((n_img * width, LANES), BF16),
+                pltpu.VMEM((n_img * width * 3 // 2, LANES), BF16),
                 pltpu.VMEM((n_img * width + 2 * GUARD, LANES), F32),
                 pltpu.VMEM((2, block, LANES), F32),
                 pltpu.VMEM((4, pairs + 3, block, LANES), BF16),
@@ -433,12 +496,13 @@
                 pltpu.VMEM((pairs + 2, padded, LANES), F32),
                 pltpu.VMEM((pairs + 2, padded, LANES), F32),
                 pltpu.VMEM((pairs * (block + 1) + 7, LANES), F32),
-                pltpu.VMEM((n_img, half, pairs, ch_b), BF16),
+                pltpu.VMEM((n_img, half, pairs, ch_b), F32),
+                pltpu.VMEM((3, 1, LANES), F32),
                 pltpu.VMEM((5, 2, LANES), F32),
                 pltpu.VMEM((5, total, 2, LANES), F32),
                 pltpu.SemaphoreType.DMA((n_chunk,)),
-                pltpu.SemaphoreType.DMA((3,)),
-                pltpu.SemaphoreType.DMA((n_out,)),
+                pltpu.SemaphoreType.DMA((6,)),
+                pltpu.SemaphoreType.DMA((n_out + 3,)),
                 pltpu.SemaphoreType.DMA((2,)),
                 pltpu.SemaphoreType.DMA((2,)),
                 pltpu.SemaphoreType.DMA((2, 2)),
@@ -449,6 +513,7 @@
             compiler_params=pltpu.CompilerParams(collective_id=0, has_side_effects=True, vmem_limit_bytes=60 * 1024 * 1024),
             name='conv_stack',
         )(images, w_a, norm_a, w_down, norm_down, w_b, norm_b)
+        result = jnp.maximum((z_val - mean[0]) * gain[0] + beta[0], 0.0).astype(BF16)
         return jnp.transpose(result, (0, 2, 1, 3))
 
     act_spec = P(('pod', 'dp'), 'sp', None, None)

time: 59.2 us -> 52.6 us (0.89)
  Pallas kernels: 56.4 us -> 49.1 us
  other arithmetic: 0 us -> 3.38 us
  local copies, waits for them, and re-layouts: 2.65 us -> 0 us
    pallas_call x1, Pallas kernels: 56.4 us -> 49.1 us  [local_stack(): pl.pallas_call(functools.partial(stack_kernel, data_size, group_size), ou...]
    transpose x0 -> x1, other arithmetic: none -> 3.38 us  [local_stack(): return jnp.transpose(result, (0, 2, 1, 3))]
    unnamed x1 -> x0, local copies, waits for them, and re-layouts: 2.65 us -> none
where the time goes in v3:
time: 52.6 us; the launch traced here: 52.4 us
  Pallas kernels  49.1 us (93%)
  other arithmetic  3.38 us (6%)
    pallas_call x1, Pallas kernels, local_stack(): pl.pallas_call(functools.partial(stack_kernel, data_size, group_size), ou...  49.1 us
    transpose x1, other arithmetic, local_stack(): return jnp.transpose(result, (0, 2, 1, 3))  3.38 us

profile of v3, /device:TPU:97, one launch (start us, length us, event | category | flops | bytes accessed | tf_op | source)
XLA Modules:
  0.0 52.4 jit_solution(1575165894629359079)
XLA Ops:
  0.0 49.1 %conv_stack.1 = (f32[12,28,16,128]{3,2,1,0:T(8,128)}, f32[1,128]{1,0:T(1,128)}, f32[1,128]{1,0:T(1,128)}, f32[1,128]{1,0:T(1,128)}) custom-call(bf16[12,32,56,64]{3,2,1,0:T(8,128)(2,1)} %images.1, bf16[2,3,3,64,64]{4,3,2,1,0:T(8,128)(2,1)} %w_a.1, f32[2,2,64]{2,1,0:T(2,128)} %norm_a.1, bf16[3,3,64,128]{3,2,1,0:T(8,128)(2,1)} %w_down.1, f32[2,128]{1,0:T(2,128)} %norm_down.1, ...), custom_call_target="tpu_custom_call" | custom-call | tf_op jit(solution)/shard_map/conv_stack/pallas_call | solution.py:471
  49.1 3.4 %fusion = bf16[12,16,28,128]{3,1,2,0:T(8,128)(2,1)} fusion(f32[12,28,16,128]{3,2,1,0:T(8,128)} %get-tuple-element.9, f32[128]{0:T(128)} %bitcast.7, f32[128]{0:T(128)} %bitcast.6, f32[128]{0:T(128)} %bitcast.5), kind=kLoop, calls=%fused_computation.1 | loop fusion | flops 3440640 | bytes 4130304 | tf_op jit(solution)/shard_map/transpose | solution.py:517

commit v4 on v3

--- a/solution.py
+++ b/solution.py
@@ -30,6 +30,8 @@
     me = dp_idx * group_size + sp_idx
     is_top = sp_idx == 0
     is_bottom = sp_idx == group_size - 1
+    keep_top = jnp.where(is_top, 0.0, 1.0).astype(F32)
+    keep_bottom = jnp.where(is_bottom, 0.0, 1.0).astype(F32)
 
     ring = group_size // 2
 
@@ -50,16 +52,17 @@
     def image_copy(idx):
         return pltpu.make_async_copy(images.at[:, pl.ds(idx * chunk, chunk)], x_in.at[:, pl.ds(idx * chunk, chunk)], in_sems.at[idx])
 
-    for idx in [0, n_chunk - 1] + list(range(1, n_chunk - 1)):
+    image_copy(0).start()
+    image_copy(n_chunk - 1).start()
+    barrier = pltpu.get_barrier_semaphore()
+    for offset in offsets:
+        pl.semaphore_signal(barrier, inc=1, device_id=peer_of(offset), device_id_type=MESH_ID)
+    for idx in range(1, n_chunk - 1):
         image_copy(idx).start()
     small_pairs = [(w_a, w_a_in), (norm_a, norm_a_in), (w_down, w_down_in), (norm_down, norm_down_in), (w_b, w_b_in), (norm_b, norm_b_in)]
     small_copies = [pltpu.make_async_copy(src, dst, w_sems.at[idx]) for idx, (src, dst) in enumerate(small_pairs)]
     for copy in small_copies:
         copy.start()
-
-    barrier = pltpu.get_barrier_semaphore()
-    for offset in offsets:
-        pl.semaphore_signal(barrier, inc=1, device_id=peer_of(offset), device_id_type=MESH_ID)
 
     pos = lax.rem(lax.broadcasted_iota(jnp.int32, (block, LANES), 0), half)
     masks[0] = (pos != 0).astype(F32)
@@ -87,14 +90,10 @@
     @pl.when(is_top)
     def _():
         from_up[...] = jnp.zeros(from_up.shape, BF16)
-        z_down[0] = jnp.zeros(z_down.shape[1:], F32)
-        z_b[0] = jnp.zeros(z_b.shape[1:], F32)
 
     @pl.when(is_bottom)
     def _():
         from_low[...] = jnp.zeros(from_low.shape, BF16)
-        z_down[pairs + 1] = jnp.zeros(z_down.shape[1:], F32)
-        z_b[pairs + 1] = jnp.zeros(z_b.shape[1:], F32)
 
     waited = set()
 
@@ -108,30 +107,52 @@
         need_row(row)
     plane = n_img * width
 
-    def two_rows(row):
-        return jnp.concatenate([x_in[:, row].astype(F32), x_in[:, row + 1].astype(F32)], axis=2).reshape(plane, LANES).astype(BF16)
-
-    send_low[...] = two_rows(rows - 2)
-    send_up[pl.ds(0, plane)] = two_rows(0)
-    third = [x_in[pl.ds(idx * (n_img // 2), n_img // 2), 2].astype(F32) for idx in range(2)]
-    send_up[pl.ds(plane, plane // 2)] = jnp.concatenate(third, axis=2).reshape(plane // 2, LANES).astype(BF16)
-
-    def image_down():
-        return pltpu.make_async_remote_copy(src_ref=send_low, dst_ref=from_up, send_sem=image_send.at[0], recv_sem=image_recv.at[0],
-                                            device_id={'sp': sp_idx + 1}, device_id_type=MESH_ID)
-
-    def image_up():
-        return pltpu.make_async_remote_copy(src_ref=send_up, dst_ref=from_low, send_sem=image_send.at[1], recv_sem=image_recv.at[1],
-                                            device_id={'sp': sp_idx - 1}, device_id_type=MESH_ID)
+    def packed_row(row):
+        halves = [x_in[pl.ds(idx * (n_img // 2), n_img // 2), row].astype(F32) for idx in range(2)]
+        return jnp.concatenate(halves, axis=2).reshape(plane // 2, LANES).astype(BF16)
+
+    for idx in range(2):
+        send_low[idx] = packed_row(rows - 1 - idx)
+    for idx in range(3):
+        send_up[idx] = packed_row(idx)
+
+    def image_copies(down, part):
+        src, dst = (send_low, from_up) if down else (send_up, from_low)
+        span = pl.ds(0, 1) if part == 0 else pl.ds(1, src.shape[0] - 1)
+        place = 2 * part + (0 if down else 1)
+        return pltpu.make_async_remote_copy(src_ref=src.at[span], dst_ref=dst.at[span], send_sem=image_send.at[place], recv_sem=image_recv.at[place],
+                                            device_id={'sp': sp_idx + 1 if down else sp_idx - 1}, device_id_type=MESH_ID)
 
     def send_images():
         @pl.when(jnp.logical_not(is_bottom))
         def _():
-            image_down().start()
+            image_copies(True, 0).start()
+            image_copies(True, 1).start()
 
         @pl.when(jnp.logical_not(is_top))
         def _():
-            image_up().start()
+            image_copies(False, 0).start()
+            image_copies(False, 1).start()
+
+    def recv_images(part):
+        @pl.when(jnp.logical_not(is_top))
+        def _():
+            image_copies(True, part).wait_recv()
+
+        @pl.when(jnp.logical_not(is_bottom))
+        def _():
+            image_copies(False, part).wait_recv()
+
+    def finish_images():
+        @pl.when(jnp.logical_not(is_bottom))
+        def _():
+            image_copies(True, 0).wait_send()
+            image_copies(True, 1).wait_send()
+
+        @pl.when(jnp.logical_not(is_top))
+        def _():
+            image_copies(False, 0).wait_send()
+            image_copies(False, 1).wait_send()
 
     ch_a = w_a.shape[3]
     zero_a = jnp.zeros((ch_a, ch_a), BF16)
@@ -167,14 +188,10 @@
         half_a = LANES // 2
         if row < -2:
             return jnp.zeros((plane, half_a), F32)
-        if row < 0:
-            return from_up[:, (row + 2) * half_a:(row + 3) * half_a].astype(F32)
-        if row < rows:
+        if 0 <= row < rows:
             need_row(row)
             return x_in[:, row].astype(F32).reshape(plane, half_a)
-        if row < rows + 2:
-            return from_low[pl.ds(0, plane), (row - rows) * half_a:(row - rows + 1) * half_a].astype(F32)
-        packed = from_low[pl.ds(plane, plane // 2), :].astype(F32)
+        packed = (from_up[-1 - row] if row < 0 else from_low[row - rows]).astype(F32)
         return jnp.concatenate([packed[:, :half_a], packed[:, half_a:]], axis=0)
 
     def spread_pair(p):
@@ -210,17 +227,12 @@
             z_last[pl.ds((2 * idx + 1) * last_stride, block)] = z_val[:, LANES:]
         return z_val
 
-    def run(n_taps, first, per, n_conv, make_taps, conv, sums):
+    def run(tap_order, conv_order, need, make_taps, conv, sums):
         made = 0
-
-        def make_until(stop):
-            nonlocal made
-            while made < min(stop, n_taps):
-                make_taps(made)
-                made += 1
-
-        for idx in range(n_conv):
-            make_until(first + idx * per)
+        for idx, count in zip(conv_order, need):
+            for tap in tap_order[made:count]:
+                make_taps(tap)
+            made = max(made, count)
             sums = conv(idx, sums)
         return sums
 
@@ -269,8 +281,6 @@
             gain, beta = gain * keep, beta * keep
         return jnp.maximum((z_val - mean) * gain + beta, 0.0)
 
-    keep_top = jnp.where(is_top, 0.0, 1.0).astype(F32)
-    keep_bottom = jnp.where(is_bottom, 0.0, 1.0).astype(F32)
     lane = lax.broadcasted_iota(jnp.int32, (1, LANES), 1)
     upper_half = (lane < LANES // 2).astype(F32)
     lower_half = 1.0 - upper_half
@@ -279,27 +289,22 @@
     widen_a(0)
 
     def conv_first(idx, acc):
-        if idx == 1:
-            pl.semaphore_wait(barrier, total - 1)
-            send_images()
-        return add_sums(acc, conv_a(0, 2 + idx, z_a))
-
-    sums = run(pairs - 1, 2, 1, pairs - 2, lambda idx: spread_pair(2 + idx), conv_first, zero_sums)
-
-    @pl.when(jnp.logical_not(is_top))
-    def _():
-        image_down().wait_recv()
-
-    spread_pair(1)
-    sums = add_sums(sums, conv_a(0, 1, z_a))
-
-    @pl.when(jnp.logical_not(is_bottom))
-    def _():
-        image_up().wait_recv()
-
-    spread_pair(pairs + 1)
-    sums = add_sums(sums, conv_a(0, pairs, z_a))
+        return add_sums(acc, conv_a(0, idx, z_a))
+
+    early = (3 * chunk + 1) // 2
+    for row in (chunk, 2 * chunk):
+        need_row(row)
+    sums = run(range(2, early + 1), range(2, early), range(2, early), spread_pair, conv_first, zero_sums)
+    pl.semaphore_wait(barrier, total - 1)
+    send_images()
+    for row in range(0, rows, chunk):
+        need_row(row)
+    last = pairs - 2
+    sums = run(range(early + 1, last + 3), range(early, last + 2), range(1, last - early + 3), spread_pair, conv_first, sums)
+    recv_images(0)
+    sums = run([1, pairs + 1], [1, pairs], [1, 2], spread_pair, conv_first, sums)
     send_sums(0, fold_sums(sums))
+    recv_images(1)
     spread_pair(0)
     conv_a(0, 0, z_a)
     spread_pair(pairs + 2)
@@ -336,59 +341,38 @@
             return acc[0] + own * new[0], acc[1] + own * new[1]
         return add_sums(acc, z_val)
 
-    sums = run(pairs + 2, 2, 1, pairs + 1, lambda idx: taps_mid(idx, z_a, scale, keep_pairs(idx)), conv_second, zero_sums)
+    sums = run(range(pairs + 2), range(pairs + 1), range(2, pairs + 3), lambda idx: taps_mid(idx, z_a, scale, keep_pairs(idx)), conv_second, zero_sums)
     send_sums(1, fold_sums(sums))
     scale_mid = scales_a(group_sum(1), count_a, norm_a_in[1])
 
     def keep_staggered(idx):
         return upper_half + lower_half * keep_bottom if idx == pairs else None
 
+    def edge_copies(ref, slot):
+        below = pltpu.make_async_remote_copy(src_ref=ref.at[pairs], dst_ref=ref.at[0], send_sem=z_send.at[slot, 0], recv_sem=z_recv.at[slot, 0],
+                                             device_id={'sp': lax.rem(sp_idx + 1, group_size)}, device_id_type=MESH_ID)
+        above = pltpu.make_async_remote_copy(src_ref=ref.at[1], dst_ref=ref.at[pairs + 1], send_sem=z_send.at[slot, 1], recv_sem=z_recv.at[slot, 1],
+                                             device_id={'sp': lax.rem(sp_idx + group_size - 1, group_size)}, device_id_type=MESH_ID)
+        return below, above
+
+    def send_edges(ref, slot):
+        for copy in edge_copies(ref, slot):
+            copy.start()
+
+    def recv_edges(ref, slot):
+        for copy in edge_copies(ref, slot):
+            copy.wait_recv()
+
+    def finish_edges(ref, slot):
+        for copy in edge_copies(ref, slot):
+            copy.wait_send()
+
+    count_b = n_img * pairs * half * total
+    last = pairs // 2 - 1
     def conv_third(idx, acc):
         return add_sums(acc, conv_down(idx))
 
-    sums = run(pairs + 1, 3, 2, pairs // 2, lambda idx: taps_mid(idx, z_mid, scale_mid, keep_staggered(idx), left=False), conv_third, zero_sums)
-
-    def edge_copies(ref, slot):
-        below = pltpu.make_async_remote_copy(src_ref=ref.at[pairs], dst_ref=ref.at[0], send_sem=z_send.at[slot, 0], recv_sem=z_recv.at[slot, 0],
-                                             device_id={'sp': sp_idx + 1}, device_id_type=MESH_ID)
-        above = pltpu.make_async_remote_copy(src_ref=ref.at[1], dst_ref=ref.at[pairs + 1], send_sem=z_send.at[slot, 1], recv_sem=z_recv.at[slot, 1],
-                                             device_id={'sp': sp_idx - 1}, device_id_type=MESH_ID)
-        return below, above
-
-    def send_edges(ref, slot):
-        below, above = edge_copies(ref, slot)
-
-        @pl.when(jnp.logical_not(is_bottom))
-        def _():
-            below.start()
-
-        @pl.when(jnp.logical_not(is_top))
-        def _():
-            above.start()
-
-    def recv_edges(ref, slot):
-        below, above = edge_copies(ref, slot)
-
-        @pl.when(jnp.logical_not(is_top))
-        def _():
-            below.wait_recv()
-
-        @pl.when(jnp.logical_not(is_bottom))
-        def _():
-            above.wait_recv()
-
-    def finish_edges(ref, slot):
-        below, above = edge_copies(ref, slot)
-
-        @pl.when(jnp.logical_not(is_bottom))
-        def _():
-            below.wait_send()
-
-        @pl.when(jnp.logical_not(is_top))
-        def _():
-            above.wait_send()
-
-    count_b = n_img * pairs * half * total
+    sums = run(range(pairs + 1), range(last + 1), range(3, pairs + 2, 2), lambda idx: taps_mid(idx, z_mid, scale_mid, keep_staggered(idx), left=False), conv_third, zero_sums)
     send_sums(2, fold_sums(sums))
     send_edges(z_down, 0)
     scale_down = scales(group_sum(2), count_b, norm_down_in[0:1], norm_down_in[1:2])
@@ -406,12 +390,12 @@
     def conv_fifth(idx, acc):
         return add_sums(acc, conv_b(1, idx))
 
-    sums = run(pairs + 2, 4, 2, pairs // 2, lambda idx: taps_low(idx, z_down, scale_down), conv_fourth, zero_sums)
+    sums = run(range(pairs + 2), range(last + 1), range(4, pairs + 3, 2), lambda idx: taps_low(idx, z_down, scale_down), conv_fourth, zero_sums)
     send_sums(3, fold_sums(sums))
     send_edges(z_b, 1)
     scale_b = scales(group_sum(3), count_b, norm_b_in[0, 0:1], norm_b_in[0, 1:2])
     recv_edges(z_b, 1)
-    sums = run(pairs + 2, 4, 2, pairs // 2, lambda idx: taps_low(idx, z_b, scale_b), conv_fifth, zero_sums)
+    sums = run(range(pairs + 2), range(last + 1), range(4, pairs + 3, 2), lambda idx: taps_low(idx, z_b, scale_b), conv_fifth, zero_sums)
     send_sums(4, fold_sums(sums))
 
     n_out = out_sems.shape[0] - 3
@@ -437,14 +421,7 @@
     for copy in scale_copies:
         copy.start()
 
-    @pl.when(jnp.logical_not(is_bottom))
-    def _():
-        image_down().wait_send()
-
-    @pl.when(jnp.logical_not(is_top))
-    def _():
-        image_up().wait_send()
-
+    finish_images()
     finish_edges(z_down, 0)
     finish_edges(z_b, 1)
     for layer in range(5):
@@ -452,6 +429,25 @@
     for idx in range(n_out):
         out_copy(idx).wait()
     for copy in scale_copies:
+        copy.wait()
+
+
+def norm_kernel(z_hbm, mean_hbm, gain_hbm, beta_hbm, out_hbm, z_ref, rows_ref, out_ref, z_sems, row_sems, out_sems):
+    n_step = z_sems.shape[0]
+    size = z_ref.shape[0] // n_step
+    row_copies = [pltpu.make_async_copy(src, rows_ref.at[idx], row_sems.at[idx]) for idx, src in enumerate((mean_hbm, gain_hbm, beta_hbm))]
+    parts = [pl.ds(idx * size, size) for idx in range(n_step)]
+    z_copies = [pltpu.make_async_copy(z_hbm.at[part], z_ref.at[part], z_sems.at[idx]) for idx, part in enumerate(parts)]
+    out_copies = [pltpu.make_async_copy(out_ref.at[part], out_hbm.at[part], out_sems.at[idx]) for idx, part in enumerate(parts)]
+    for copy in row_copies + z_copies:
+        copy.start()
+    for copy in row_copies:
+        copy.wait()
+    for part, z_copy, out_copy in zip(parts, z_copies, out_copies):
+        z_copy.wait()
+        out_ref[part] = jnp.maximum((z_ref[part] - rows_ref[0]) * rows_ref[1] + rows_ref[2], 0.0).astype(BF16)
+        out_copy.start()
+    for copy in out_copies:
         copy.wait()
 
 
@@ -484,10 +480,10 @@
                 pltpu.VMEM((2, 16 * ch_a, 2 * LANES), BF16),
                 pltpu.VMEM((18 * ch_a, 2 * LANES), BF16),
                 pltpu.VMEM((2, 12 * ch_b, 2 * LANES), BF16),
-                pltpu.VMEM((n_img * width, LANES), BF16),
-                pltpu.VMEM((n_img * width * 3 // 2, LANES), BF16),
-                pltpu.VMEM((n_img * width, LANES), BF16),
-                pltpu.VMEM((n_img * width * 3 // 2, LANES), BF16),
+                pltpu.VMEM((2, n_img * width // 2, LANES), BF16),
+                pltpu.VMEM((3, n_img * width // 2, LANES), BF16),
+                pltpu.VMEM((2, n_img * width // 2, LANES), BF16),
+                pltpu.VMEM((3, n_img * width // 2, LANES), BF16),
                 pltpu.VMEM((n_img * width + 2 * GUARD, LANES), F32),
                 pltpu.VMEM((2, block, LANES), F32),
                 pltpu.VMEM((4, pairs + 3, block, LANES), BF16),
@@ -503,8 +499,8 @@
                 pltpu.SemaphoreType.DMA((n_chunk,)),
                 pltpu.SemaphoreType.DMA((6,)),
                 pltpu.SemaphoreType.DMA((n_out + 3,)),
-                pltpu.SemaphoreType.DMA((2,)),
-                pltpu.SemaphoreType.DMA((2,)),
+                pltpu.SemaphoreType.DMA((4,)),
+                pltpu.SemaphoreType.DMA((4,)),
                 pltpu.SemaphoreType.DMA((2, 2)),
                 pltpu.SemaphoreType.DMA((2, 2)),
                 pltpu.SemaphoreType.DMA((5,)),
@@ -513,7 +509,23 @@
             compiler_params=pltpu.CompilerParams(collective_id=0, has_side_effects=True, vmem_limit_bytes=60 * 1024 * 1024),
             name='conv_stack',
         )(images, w_a, norm_a, w_down, norm_down, w_b, norm_b)
-        result = jnp.maximum((z_val - mean[0]) * gain[0] + beta[0], 0.0).astype(BF16)
+        n_step = 6
+        result = pl.pallas_call(
+            norm_kernel,
+            out_shape=jax.ShapeDtypeStruct(z_val.shape, BF16),
+            in_specs=[any_spec] * 4,
+            out_specs=any_spec,
+            scratch_shapes=[
+                pltpu.VMEM(z_val.shape, F32),
+                pltpu.VMEM((3, 1, ch_b), F32),
+                pltpu.VMEM(z_val.shape, BF16),
+                pltpu.SemaphoreType.DMA((n_step,)),
+                pltpu.SemaphoreType.DMA((3,)),
+                pltpu.SemaphoreType.DMA((n_step,)),
+            ],
+            compiler_params=pltpu.CompilerParams(vmem_limit_bytes=60 * 1024 * 1024),
+            name='last_norm',
+        )(z_val, mean, gain, beta)
         return jnp.transpose(result, (0, 2, 1, 3))
 
     act_spec = P(('pod', 'dp'), 'sp', None, None)

time: 52.6 us -> 51 us (0.970)
  other arithmetic: 3.38 us -> 0 us
  Pallas kernels: 49.1 us -> 50.7 us
    transpose x1 -> x0, other arithmetic: 3.38 us -> none  [local_stack(): return jnp.transpose(result, (0, 2, 1, 3))]
    pallas_call x0 -> x1, Pallas kernels: none -> 2.61 us  [local_stack(): pl.pallas_call(norm_kernel, out_shape=jax.ShapeDtypeStruct(z_val.shape, B...]
    pallas_call x1, Pallas kernels: 49.1 us -> 48.1 us  [local_stack(): pl.pallas_call(functools.partial(stack_kernel, data_size, group_size), ou...]
where the time goes in v4:
time: 51 us; the launch traced here: 50.9 us
  Pallas kernels  50.7 us (99%)
    pallas_call x1, Pallas kernels, local_stack(): pl.pallas_call(functools.partial(stack_kernel, data_size, group_size), ou...  48.1 us
    pallas_call x1, Pallas kernels, local_stack(): pl.pallas_call(norm_kernel, out_shape=jax.ShapeDtypeStruct(z_val.shape, B...  2.61 us

profile of v4, /device:TPU:97, one launch (start us, length us, event | category | flops | bytes accessed | tf_op | source)
XLA Modules:
  0.0 50.9 jit_solution(10749348430161689409)
XLA Ops:
  0.0 48.1 %conv_stack.1 = (f32[12,28,16,128]{3,2,1,0:T(8,128)}, f32[1,128]{1,0:T(1,128)}, f32[1,128]{1,0:T(1,128)}, f32[1,128]{1,0:T(1,128)}) custom-call(bf16[12,32,56,64]{3,2,1,0:T(8,128)(2,1)} %images.1, bf16[2,3,3,64,64]{4,3,2,1,0:T(8,128)(2,1)} %w_a.1, f32[2,2,64]{2,1,0:T(2,128)} %norm_a.1, bf16[3,3,64,128]{3,2,1,0:T(8,128)(2,1)} %w_down.1, f32[2,128]{1,0:T(2,128)} %norm_down.1, ...), custom_call_target="tpu_custom_call" | custom-call | tf_op jit(solution)/shard_map/conv_stack/pallas_call | solution.py:467
  48.1 2.6 %last_norm.1 = bf16[12,28,16,128]{3,2,1,0:T(8,128)(2,1)} custom-call(f32[12,28,16,128]{3,2,1,0:T(8,128)} %get-tuple-element.9.z_hbm, f32[1,128]{1,0:T(1,128)} %get-tuple-element.10.mean_hbm, f32[1,128]{1,0:T(1,128)} %get-tuple-element.11.gain_hbm, f32[1,128]{1,0:T(1,128)} %get-tuple-element.12.beta_hbm), custom_call_target="tpu_custom_call" | custom-call | tf_op jit(solution)/shard_map/last_norm/pallas_call | solution.py:513

commit v5 on v4

--- a/solution.py
+++ b/solution.py
@@ -291,9 +291,7 @@
     def conv_first(idx, acc):
         return add_sums(acc, conv_a(0, idx, z_a))
 
-    early = (3 * chunk + 1) // 2
-    for row in (chunk, 2 * chunk):
-        need_row(row)
+    early = chunk // 2
     sums = run(range(2, early + 1), range(2, early), range(2, early), spread_pair, conv_first, zero_sums)
     pl.semaphore_wait(barrier, total - 1)
     send_images()
@@ -463,7 +461,7 @@
         block = n_img * half
         padded = block + 2 * GUARD
         any_spec = pl.BlockSpec(memory_space=pl.ANY)
-        n_chunk, n_out = 8, 4
+        n_chunk, n_out = 4, 4
         z_val, mean, gain, beta = pl.pallas_call(
             functools.partial(stack_kernel, data_size, group_size),
             out_shape=(jax.ShapeDtypeStruct((n_img, half, pairs, ch_b), F32),) + (jax.ShapeDtypeStruct((1, LANES), F32),) * 3,

time: 51 us -> 50.6 us (level)
  no operation moved by 1% of the time
where the time goes in v5:
time: 50.6 us; the launch traced here: 50.5 us
  Pallas kernels  50.3 us (99%)
    pallas_call x1, Pallas kernels, local_stack(): pl.pallas_call(functools.partial(stack_kernel, data_size, group_size), ou...  47.7 us
    pallas_call x1, Pallas kernels, local_stack(): pl.pallas_call(norm_kernel, out_shape=jax.ShapeDtypeStruct(z_val.shape, B...  2.61 us

profile of v5, /device:TPU:97, one launch (start us, length us, event | category | flops | bytes accessed | tf_op | source)
XLA Modules:
  0.0 50.5 jit_solution(16445991185855331768)
XLA Ops:
  0.0 47.7 %conv_stack.1 = (f32[12,28,16,128]{3,2,1,0:T(8,128)}, f32[1,128]{1,0:T(1,128)}, f32[1,128]{1,0:T(1,128)}, f32[1,128]{1,0:T(1,128)}) custom-call(bf16[12,32,56,64]{3,2,1,0:T(8,128)(2,1)} %images.1, bf16[2,3,3,64,64]{4,3,2,1,0:T(8,128)(2,1)} %w_a.1, f32[2,2,64]{2,1,0:T(2,128)} %norm_a.1, bf16[3,3,64,128]{3,2,1,0:T(8,128)(2,1)} %w_down.1, f32[2,128]{1,0:T(2,128)} %norm_down.1, ...), custom_call_target="tpu_custom_call" | custom-call | tf_op jit(solution)/shard_map/conv_stack/pallas_call | solution.py:465
  47.7 2.6 %last_norm.1 = bf16[12,28,16,128]{3,2,1,0:T(8,128)(2,1)} custom-call(f32[12,28,16,128]{3,2,1,0:T(8,128)} %get-tuple-element.9.z_hbm, f32[1,128]{1,0:T(1,128)} %get-tuple-element.10.mean_hbm, f32[1,128]{1,0:T(1,128)} %get-tuple-element.11.gain_hbm, f32[1,128]{1,0:T(1,128)} %get-tuple-element.12.beta_hbm), custom_call_target="tpu_custom_call" | custom-call | tf_op jit(solution)/shard_map/last_norm/pallas_call | solution.py:511

commit v6 on v5

--- a/solution.py
+++ b/solution.py
@@ -374,7 +374,6 @@
     send_sums(2, fold_sums(sums))
     send_edges(z_down, 0)
     scale_down = scales(group_sum(2), count_b, norm_down_in[0:1], norm_down_in[1:2])
-    recv_edges(z_down, 0)
 
     def taps_low(idx, src, scale):
         keep = keep_pairs(idx)
@@ -388,12 +387,20 @@
     def conv_fifth(idx, acc):
         return add_sums(acc, conv_b(1, idx))
 
-    sums = run(range(pairs + 2), range(last + 1), range(4, pairs + 3, 2), lambda idx: taps_low(idx, z_down, scale_down), conv_fourth, zero_sums)
+    inner_taps = list(range(2, pairs)) + [1, pairs]
+    inner_need = list(range(4, pairs - 3, 2)) + [pairs]
+
+    def run_low(src, slot, scale, conv):
+        make = lambda idx: taps_low(idx, src, scale)
+        acc = run(inner_taps, range(1, last), inner_need, make, conv, zero_sums)
+        recv_edges(src, slot)
+        return run([0, pairs + 1], [0, last], [1, 2], make, conv, acc)
+
+    sums = run_low(z_down, 0, scale_down, conv_fourth)
     send_sums(3, fold_sums(sums))
     send_edges(z_b, 1)
     scale_b = scales(group_sum(3), count_b, norm_b_in[0, 0:1], norm_b_in[0, 1:2])
-    recv_edges(z_b, 1)
-    sums = run(range(pairs + 2), range(last + 1), range(4, pairs + 3, 2), lambda idx: taps_low(idx, z_b, scale_b), conv_fifth, zero_sums)
+    sums = run_low(z_b, 1, scale_b, conv_fifth)
     send_sums(4, fold_sums(sums))
 
     n_out = out_sems.shape[0] - 3

time: 50.6 us -> 50.3 us (level)
  no operation moved by 1% of the time
where the time goes in v6:
time: 50.3 us; the launch traced here: 50.2 us
  Pallas kernels  50 us (99%)
    pallas_call x1, Pallas kernels, local_stack(): pl.pallas_call(functools.partial(stack_kernel, data_size, group_size), ou...  47.4 us
    pallas_call x1, Pallas kernels, local_stack(): pl.pallas_call(norm_kernel, out_shape=jax.ShapeDtypeStruct(z_val.shape, B...  2.61 us

profile of v6, /device:TPU:97, one launch (start us, length us, event | category | flops | bytes accessed | tf_op | source)
XLA Modules:
  0.0 50.2 jit_solution(12639649151877076757)
XLA Ops:
  0.0 47.4 %conv_stack.1 = (f32[12,28,16,128]{3,2,1,0:T(8,128)}, f32[1,128]{1,0:T(1,128)}, f32[1,128]{1,0:T(1,128)}, f32[1,128]{1,0:T(1,128)}) custom-call(bf16[12,32,56,64]{3,2,1,0:T(8,128)(2,1)} %images.1, bf16[2,3,3,64,64]{4,3,2,1,0:T(8,128)(2,1)} %w_a.1, f32[2,2,64]{2,1,0:T(2,128)} %norm_a.1, bf16[3,3,64,128]{3,2,1,0:T(8,128)(2,1)} %w_down.1, f32[2,128]{1,0:T(2,128)} %norm_down.1, ...), custom_call_target="tpu_custom_call" | custom-call | tf_op jit(solution)/shard_map/conv_stack/pallas_call | solution.py:472
  47.4 2.6 %last_norm.1 = bf16[12,28,16,128]{3,2,1,0:T(8,128)(2,1)} custom-call(f32[12,28,16,128]{3,2,1,0:T(8,128)} %get-tuple-element.9.z_hbm, f32[1,128]{1,0:T(1,128)} %get-tuple-element.10.mean_hbm, f32[1,128]{1,0:T(1,128)} %get-tuple-element.11.gain_hbm, f32[1,128]{1,0:T(1,128)} %get-tuple-element.12.beta_hbm), custom_call_target="tpu_custom_call" | custom-call | tf_op jit(solution)/shard_map/last_norm/pallas_call | solution.py:518
